TPU v7x, 8 devices: a whole 2x2x1 slice. The times are simulated.
8 devices in a mesh: dp: 2 (over z, y), pp: 4 (over x, core).
Axes of the slice: x: 2, y: 2, z: 1, core: 2. Of those that a mesh axis runs over, the one named last changes fastest.
Arguments:
- x_in: bfloat16 [6, 8, 128, 2432], P('dp'), parts along dimension 0
- cond_vec: bfloat16 [6, 2432], P('dp'), parts along dimension 0
- pos_ids: int32 [8, 128, 3], replicated
- w_mod: bfloat16 [4, 2432, 7296], P('pp')
- b_mod: bfloat16 [4, 7296], P('pp')
- w_one: bfloat16 [4, 2432, 17024], P('pp')
- b_one: bfloat16 [4, 17024], P('pp')
- qk_scale: bfloat16 [4, 2, 64], P('pp')
- w_two: bfloat16 [4, 12160, 2432], P('pp')
- b_two: bfloat16 [4, 2432], P('pp')
- k_prev: bfloat16 [4, 6, 8, 128, 2432], P('pp', 'dp'), parts along dimension 1
- v_prev: bfloat16 [4, 6, 8, 128, 2432], P('pp', 'dp'), parts along dimension 1
Outputs:
- output 1: bfloat16 [6, 8, 128, 2432], P('dp', 'pp'), parts along dimension 0
- output 2: bfloat16 [4, 6, 8, 128, 2432], P('pp', 'dp'), parts along dimension 1
- output 3: bfloat16 [4, 6, 8, 128, 2432], P('pp', 'dp'), parts along dimension 1
There are 2 independent parts. A program takes and returns all parts, laid end to end along the dimension named above; an argument that names none is the same for every part.
All inputs are finite; a program needn't handle non-finite values.
Results may differ from a plain program's by a relative error of at most 0.0108307.
Values are sent between devices in bfloat16 or wider.
A program may use at most 1 GiB of HBM per device.

v0:
```python
import math
import jax
import jax.numpy as jnp
from jax import lax
from jax.sharding import PartitionSpec as P


def layer_norm(hidden):
    act32 = hidden.astype(jnp.float32)
    centered = act32 - jnp.mean(act32, axis=-1, keepdims=True)
    return centered * lax.rsqrt(jnp.mean(centered * centered, axis=-1, keepdims=True) + 1e-6)


def rope_tables(pos_ids, head_dim):
    axis_zero = head_dim // 8
    axis_rest = (head_dim - axis_zero) // 2
    pieces = []
    for axis_idx, axis_dim in enumerate((axis_zero, axis_rest, head_dim - axis_zero - axis_rest)):
        axis_freqs = 1.0 / (10000.0 ** (jnp.arange(0, axis_dim, 2, dtype=jnp.float32) / axis_dim))
        pieces.append(pos_ids[..., axis_idx:axis_idx + 1].astype(jnp.float32) * axis_freqs)
    angles = jnp.concatenate(pieces, axis=-1)[..., None, :]
    return jnp.cos(angles), jnp.sin(angles)


def rms_rope(raw_heads, norm_gain, cos_tab, sin_tab):
    raw32 = raw_heads.astype(jnp.float32)
    normed = raw32 * lax.rsqrt(jnp.mean(raw32 * raw32, axis=-1, keepdims=True) + 1e-6) * norm_gain.astype(jnp.float32)
    pair_view = normed.reshape(normed.shape[:-1] + (normed.shape[-1] // 2, 2))
    even_part = pair_view[..., 0]
    odd_part = pair_view[..., 1]
    rotated = jnp.stack([cos_tab * even_part - sin_tab * odd_part, sin_tab * even_part + cos_tab * odd_part], axis=-1)
    return rotated.reshape(raw_heads.shape).astype(jnp.bfloat16)


def solution(mesh):
    stages = mesh.shape['pp']
    send_pairs = [(src_stage, src_stage + 1) for src_stage in range(stages - 1)]

    def stage_program(x_in, cond_vec, pos_ids, w_mod, b_mod, w_one, b_one, qk_scale, w_two, b_two, k_prev, v_prev):
        batch_size, patches, patch_tok, width = x_in.shape
        stage_layers = w_one.shape[0]
        head_dim = qk_scale.shape[-1]
        head_count = width // head_dim
        seq_len = patches * patch_tok
        score_scale = 1.0 / math.sqrt(head_dim)
        head_shape = (batch_size, patch_tok, head_count, head_dim)
        stage_idx = lax.axis_index('pp')
        cond_act = jax.nn.silu(cond_vec.astype(jnp.float32)).astype(jnp.bfloat16)
        mod_all = jnp.einsum('bd,lde->lbe', cond_act, w_mod, preferred_element_type=jnp.float32) + b_mod[:, None, :].astype(jnp.float32)
        cos_all, sin_all = rope_tables(pos_ids, head_dim)

        def run_patch(hidden, patch_idx, k_buf, v_buf):
            cos_tab = lax.dynamic_index_in_dim(cos_all, patch_idx, axis=0, keepdims=False)
            sin_tab = lax.dynamic_index_in_dim(sin_all, patch_idx, axis=0, keepdims=False)
            for layer_idx in range(stage_layers):
                mod_vals = mod_all[layer_idx][:, None, :]
                shift_mod = mod_vals[..., :width]
                scale_mod = mod_vals[..., width:2 * width]
                gate_mod = mod_vals[..., 2 * width:]
                h_mod = (layer_norm(hidden) * (1.0 + scale_mod) + shift_mod).astype(jnp.bfloat16)
                proj_out = (jnp.einsum('btd,de->bte', h_mod, w_one[layer_idx], preferred_element_type=jnp.float32) + b_one[layer_idx].astype(jnp.float32)).astype(jnp.bfloat16)
                q_rot = rms_rope(proj_out[..., :width].reshape(head_shape), qk_scale[layer_idx, 0], cos_tab, sin_tab)
                k_rot = rms_rope(proj_out[..., width:2 * width].reshape(head_shape), qk_scale[layer_idx, 1], cos_tab, sin_tab)
                v_fresh = proj_out[..., 2 * width:3 * width]
                k_buf = lax.dynamic_update_slice(k_buf, k_rot.reshape(1, batch_size, 1, patch_tok, width), (layer_idx, 0, patch_idx, 0, 0))
                v_buf = lax.dynamic_update_slice(v_buf, v_fresh.reshape(1, batch_size, 1, patch_tok, width), (layer_idx, 0, patch_idx, 0, 0))
                key_all = k_buf[layer_idx].reshape(batch_size, seq_len, head_count, head_dim)
                val_all = v_buf[layer_idx].reshape(batch_size, seq_len, head_count, head_dim)
                scores = jnp.einsum('bqhd,bkhd->bhqk', q_rot, key_all, preferred_element_type=jnp.float32) * score_scale
                prob_bf = jax.nn.softmax(scores, axis=-1).astype(jnp.bfloat16)
                attn_out = jnp.einsum('bhqk,bkhd->bqhd', prob_bf, val_all, preferred_element_type=jnp.float32).astype(jnp.bfloat16).reshape(batch_size, patch_tok, width)
                mlp_act = jax.nn.gelu(proj_out[..., 3 * width:].astype(jnp.float32), approximate=True).astype(jnp.bfloat16)
                joined = jnp.concatenate([attn_out, mlp_act], axis=-1)
                block_out = jnp.einsum('bte,ed->btd', joined, w_two[layer_idx], preferred_element_type=jnp.float32) + b_two[layer_idx].astype(jnp.float32)
                hidden = (hidden.astype(jnp.float32) + gate_mod * block_out).astype(jnp.bfloat16)
            return hidden, k_buf, v_buf

        def skip_patch(hidden, patch_idx, k_buf, v_buf):
            return hidden, k_buf, v_buf

        def step_body(step_idx, loop_carry):
            recv_act, k_buf, v_buf, out_acc = loop_carry
            patch_idx = step_idx - stage_idx
            is_valid = (patch_idx >= 0) & (patch_idx < patches)
            safe_idx = jnp.clip(patch_idx, 0, patches - 1)
            first_in = lax.dynamic_index_in_dim(x_in, safe_idx, axis=1, keepdims=False)
            hidden = jnp.where(stage_idx == 0, first_in, recv_act)
            hidden, k_buf, v_buf = lax.cond(is_valid, run_patch, skip_patch, hidden, safe_idx, k_buf, v_buf)
            old_slot = lax.dynamic_index_in_dim(out_acc, safe_idx, axis=1, keepdims=False)
            new_slot = jnp.where(is_valid & (stage_idx == stages - 1), hidden, old_slot)
            out_acc = lax.dynamic_update_index_in_dim(out_acc, new_slot, safe_idx, axis=1)
            recv_act = lax.ppermute(hidden, 'pp', send_pairs)
            return recv_act, k_buf, v_buf, out_acc

        init_carry = (jnp.zeros((batch_size, patch_tok, width), jnp.bfloat16), k_prev, v_prev, jnp.zeros_like(x_in))
        recv_act, k_new, v_new, out_acc = lax.fori_loop(0, patches + stages - 1, step_body, init_carry)
        last_only = jnp.where(stage_idx == stages - 1, out_acc, jnp.zeros_like(out_acc))
        x_out = lax.psum_scatter(last_only, 'pp', scatter_dimension=1, tiled=True)
        return x_out, k_new, v_new

    return jax.shard_map(
        stage_program, mesh=mesh,
        in_specs=(P('dp'), P('dp'), P(), P('pp'), P('pp'), P('pp'), P('pp'), P('pp'), P('pp'), P('pp'), P('pp', 'dp'), P('pp', 'dp')),
        out_specs=(P('dp', 'pp'), P('pp', 'dp'), P('pp', 'dp')),
        check_vma=False)
```

profile of v0, /device:TPU:7, one launch (start us, length us, event | category | flops | bytes accessed | tf_op | source)
XLA Modules:
  0.0 5943.2 jit_solution(13732295173865088822)
XLA Ops:
  72.4 5595.6 %while.20 = (s32[]{:T(128)}, bf16[3,128,2432]{2,1,0:T(8,128)(2,1)S(1)}, bf16[1,3,8,128,2432]{3,2,4,1,0:T(8,128)(2,1)}, bf16[1,3,8,128,2432]{3,2,4,1,0:T(8,128)(2...) while((s32[]{:T(128)}, ...), condition=%wide.region_9.10_spmd, body=%wide.region_0.9_spmd.sunk | while | flops 58523082752 | bytes 541216064 | solution.py:96
  116.9 1455.7 %collective-permute-done = bf16[3,128,2432]{2,1,0:T(8,128)(2,1)S(1)} collective-permute-done((bf16[3,128,2432]{2,1,0:T(8,128)(2,1)}, bf16[3,128,2432]{2,1,0:T(8,128)(2,1)S(1)}, u32[]{:S(2)}, u32[]{:S(2)}) %collective-permute-start) | collective-permute-done | bytes 1867808 | tf_op jit(solution)/shard_map/while/body/eval_jaxpr/ppermute | solution.py:92
  1575.6 485.3 %conditional.2 = ((bf16[3,128,2432]{2,1,0:T(8,128)(2,1)}, bf16[1,3,8,128,2432]{3,2,4,1,0:T(8,128)(2,1)}, bf16[1,3,8,128,2432]{3,2,4,1,0:T(8,128)(2,1)})) conditional(s32[]{:T(128)} %convert_element_type.234, (bf16[3,128,2432]{2,1,0:T(8,128)(2,1)}, bf16[1,3,8,128,2432]{3,2,4,1,0:T(8,128)(2,1)}, bf16[1,3,8,128,2432]{3,2,4,1,0:T(8,128)(2,1)}) %tuple.71, ...), branch_computations={%region_1.1_spmd, %region_2.8_spmd} | conditional | flops 58521214976 | bytes 518665632 | solution.py:88
  1581.2 45.4 add_convert_fusion
  1707.2 95.9 %dynamic_update_slice.13 = bf16[1,3,8,128,2432]{3,2,4,1,0:T(8,128)(2,1)} dynamic-update-slice(bf16[1,3,8,128,2432]{3,2,4,1,0:T(8,128)(2,1)} %get-tuple-element.444, bf16[1,3,1,128,2432]{3,2,4,1,0:T(2,128)(2,1)} %copy.55, s32[]{:T(128)} %constant.98.clone, s32[]{:T(128)} %constant.98.clone, s32[]{:T(128)S(6)} %select_n.49, s32[]{:T(128)} %constant.98.clone, s32[]{:T(128)} %constant.98.clone) | dynamic-update-slice | bytes 3735556 | tf_op jit(solution)/shard_map/while/body/eval_jaxpr/cond/branch_1_fun/dynamic_update_slice | solution.py:65
  1833.8 30.2 fusion.78
  1870.2 95.9 %dynamic_update_slice.12 = bf16[1,3,8,128,2432]{3,2,4,1,0:T(8,128)(2,1)} dynamic-update-slice(bf16[1,3,8,128,2432]{3,2,4,1,0:T(8,128)(2,1)} %get-tuple-element.440, bf16[1,3,1,128,2432]{3,2,4,1,0:T(2,128)(2,1)} %copy.49, s32[]{:T(128)} %constant.98.clone, s32[]{:T(128)} %constant.98.clone, s32[]{:T(128)S(6)} %select_n.49, s32[]{:T(128)} %constant.98.clone, s32[]{:T(128)} %constant.98.clone) | dynamic-update-slice | bytes 3735556 | tf_op jit(solution)/shard_map/while/body/eval_jaxpr/cond/branch_1_fun/dynamic_update_slice | solution.py:66
  2027.9 32.8 fusion.39
  2089.7 485.8 %conditional.2 = ((bf16[3,128,2432]{2,1,0:T(8,128)(2,1)}, bf16[1,3,8,128,2432]{3,2,4,1,0:T(8,128)(2,1)}, bf16[1,3,8,128,2432]{3,2,4,1,0:T(8,128)(2,1)})) conditional(s32[]{:T(128)} %convert_element_type.234, (bf16[3,128,2432]{2,1,0:T(8,128)(2,1)}, bf16[1,3,8,128,2432]{3,2,4,1,0:T(8,128)(2,1)}, bf16[1,3,8,128,2432]{3,2,4,1,0:T(8,128)(2,1)}) %tuple.71, ...), branch_computations={%region_1.1_spmd, %region_2.8_spmd} | conditional | flops 58521214976 | bytes 518665632 | solution.py:88
  2095.4 45.4 add_convert_fusion
  2221.6 95.9 %dynamic_update_slice.13 = bf16[1,3,8,128,2432]{3,2,4,1,0:T(8,128)(2,1)} dynamic-update-slice(bf16[1,3,8,128,2432]{3,2,4,1,0:T(8,128)(2,1)} %get-tuple-element.444, bf16[1,3,1,128,2432]{3,2,4,1,0:T(2,128)(2,1)} %copy.55, s32[]{:T(128)} %constant.98.clone, s32[]{:T(128)} %constant.98.clone, s32[]{:T(128)S(6)} %select_n.49, s32[]{:T(128)} %constant.98.clone, s32[]{:T(128)} %constant.98.clone) | dynamic-update-slice | bytes 3735556 | tf_op jit(solution)/shard_map/while/body/eval_jaxpr/cond/branch_1_fun/dynamic_update_slice | solution.py:65
  2384.6 95.9 %dynamic_update_slice.12 = bf16[1,3,8,128,2432]{3,2,4,1,0:T(8,128)(2,1)} dynamic-update-slice(bf16[1,3,8,128,2432]{3,2,4,1,0:T(8,128)(2,1)} %get-tuple-element.440, bf16[1,3,1,128,2432]{3,2,4,1,0:T(2,128)(2,1)} %copy.49, s32[]{:T(128)} %constant.98.clone, s32[]{:T(128)} %constant.98.clone, s32[]{:T(128)S(6)} %select_n.49, s32[]{:T(128)} %constant.98.clone, s32[]{:T(128)} %constant.98.clone) | dynamic-update-slice | bytes 3735556 | tf_op jit(solution)/shard_map/while/body/eval_jaxpr/cond/branch_1_fun/dynamic_update_slice | solution.py:66
  2542.3 32.8 fusion.39
  2603.3 485.7 %conditional.2 = ((bf16[3,128,2432]{2,1,0:T(8,128)(2,1)}, bf16[1,3,8,128,2432]{3,2,4,1,0:T(8,128)(2,1)}, bf16[1,3,8,128,2432]{3,2,4,1,0:T(8,128)(2,1)})) conditional(s32[]{:T(128)} %convert_element_type.234, (bf16[3,128,2432]{2,1,0:T(8,128)(2,1)}, bf16[1,3,8,128,2432]{3,2,4,1,0:T(8,128)(2,1)}, bf16[1,3,8,128,2432]{3,2,4,1,0:T(8,128)(2,1)}) %tuple.71, ...), branch_computations={%region_1.1_spmd, %region_2.8_spmd} | conditional | flops 58521214976 | bytes 518665632 | solution.py:88
  2608.9 45.4 add_convert_fusion
  2735.4 95.9 %dynamic_update_slice.13 = bf16[1,3,8,128,2432]{3,2,4,1,0:T(8,128)(2,1)} dynamic-update-slice(bf16[1,3,8,128,2432]{3,2,4,1,0:T(8,128)(2,1)} %get-tuple-element.444, bf16[1,3,1,128,2432]{3,2,4,1,0:T(2,128)(2,1)} %copy.55, s32[]{:T(128)} %constant.98.clone, s32[]{:T(128)} %constant.98.clone, s32[]{:T(128)S(6)} %select_n.49, s32[]{:T(128)} %constant.98.clone, s32[]{:T(128)} %constant.98.clone) | dynamic-update-slice | bytes 3735556 | tf_op jit(solution)/shard_map/while/body/eval_jaxpr/cond/branch_1_fun/dynamic_update_slice | solution.py:65
  2862.0 30.2 fusion.78
  2898.4 95.9 %dynamic_update_slice.12 = bf16[1,3,8,128,2432]{3,2,4,1,0:T(8,128)(2,1)} dynamic-update-slice(bf16[1,3,8,128,2432]{3,2,4,1,0:T(8,128)(2,1)} %get-tuple-element.440, bf16[1,3,1,128,2432]{3,2,4,1,0:T(2,128)(2,1)} %copy.49, s32[]{:T(128)} %constant.98.clone, s32[]{:T(128)} %constant.98.clone, s32[]{:T(128)S(6)} %select_n.49, s32[]{:T(128)} %constant.98.clone, s32[]{:T(128)} %constant.98.clone) | dynamic-update-slice | bytes 3735556 | tf_op jit(solution)/shard_map/while/body/eval_jaxpr/cond/branch_1_fun/dynamic_update_slice | solution.py:66
  3056.0 32.8 fusion.39
  3117.5 485.8 %conditional.2 = ((bf16[3,128,2432]{2,1,0:T(8,128)(2,1)}, bf16[1,3,8,128,2432]{3,2,4,1,0:T(8,128)(2,1)}, bf16[1,3,8,128,2432]{3,2,4,1,0:T(8,128)(2,1)})) conditional(s32[]{:T(128)} %convert_element_type.234, (bf16[3,128,2432]{2,1,0:T(8,128)(2,1)}, bf16[1,3,8,128,2432]{3,2,4,1,0:T(8,128)(2,1)}, bf16[1,3,8,128,2432]{3,2,4,1,0:T(8,128)(2,1)}) %tuple.71, ...), branch_computations={%region_1.1_spmd, %region_2.8_spmd} | conditional | flops 58521214976 | bytes 518665632 | solution.py:88
  3123.1 45.4 add_convert_fusion
  3249.6 95.9 %dynamic_update_slice.13 = bf16[1,3,8,128,2432]{3,2,4,1,0:T(8,128)(2,1)} dynamic-update-slice(bf16[1,3,8,128,2432]{3,2,4,1,0:T(8,128)(2,1)} %get-tuple-element.444, bf16[1,3,1,128,2432]{3,2,4,1,0:T(2,128)(2,1)} %copy.55, s32[]{:T(128)} %constant.98.clone, s32[]{:T(128)} %constant.98.clone, s32[]{:T(128)S(6)} %select_n.49, s32[]{:T(128)} %constant.98.clone, s32[]{:T(128)} %constant.98.clone) | dynamic-update-slice | bytes 3735556 | tf_op jit(solution)/shard_map/while/body/eval_jaxpr/cond/branch_1_fun/dynamic_update_slice | solution.py:65
  3376.2 30.2 fusion.78
  3412.6 95.9 %dynamic_update_slice.12 = bf16[1,3,8,128,2432]{3,2,4,1,0:T(8,128)(2,1)} dynamic-update-slice(bf16[1,3,8,128,2432]{3,2,4,1,0:T(8,128)(2,1)} %get-tuple-element.440, bf16[1,3,1,128,2432]{3,2,4,1,0:T(2,128)(2,1)} %copy.49, s32[]{:T(128)} %constant.98.clone, s32[]{:T(128)} %constant.98.clone, s32[]{:T(128)S(6)} %select_n.49, s32[]{:T(128)} %constant.98.clone, s32[]{:T(128)} %constant.98.clone) | dynamic-update-slice | bytes 3735556 | tf_op jit(solution)/shard_map/while/body/eval_jaxpr/cond/branch_1_fun/dynamic_update_slice | solution.py:66
  3570.2 32.8 fusion.39
  3631.4 485.8 %conditional.2 = ((bf16[3,128,2432]{2,1,0:T(8,128)(2,1)}, bf16[1,3,8,128,2432]{3,2,4,1,0:T(8,128)(2,1)}, bf16[1,3,8,128,2432]{3,2,4,1,0:T(8,128)(2,1)})) conditional(s32[]{:T(128)} %convert_element_type.234, (bf16[3,128,2432]{2,1,0:T(8,128)(2,1)}, bf16[1,3,8,128,2432]{3,2,4,1,0:T(8,128)(2,1)}, bf16[1,3,8,128,2432]{3,2,4,1,0:T(8,128)(2,1)}) %tuple.71, ...), branch_computations={%region_1.1_spmd, %region_2.8_spmd} | conditional | flops 58521214976 | bytes 518665632 | solution.py:88
  3637.0 45.4 add_convert_fusion
  3763.3 95.9 %dynamic_update_slice.13 = bf16[1,3,8,128,2432]{3,2,4,1,0:T(8,128)(2,1)} dynamic-update-slice(bf16[1,3,8,128,2432]{3,2,4,1,0:T(8,128)(2,1)} %get-tuple-element.444, bf16[1,3,1,128,2432]{3,2,4,1,0:T(2,128)(2,1)} %copy.55, s32[]{:T(128)} %constant.98.clone, s32[]{:T(128)} %constant.98.clone, s32[]{:T(128)S(6)} %select_n.49, s32[]{:T(128)} %constant.98.clone, s32[]{:T(128)} %constant.98.clone) | dynamic-update-slice | bytes 3735556 | tf_op jit(solution)/shard_map/while/body/eval_jaxpr/cond/branch_1_fun/dynamic_update_slice | solution.py:65
  3889.8 30.2 fusion.78
  3926.3 95.9 %dynamic_update_slice.12 = bf16[1,3,8,128,2432]{3,2,4,1,0:T(8,128)(2,1)} dynamic-update-slice(bf16[1,3,8,128,2432]{3,2,4,1,0:T(8,128)(2,1)} %get-tuple-element.440, bf16[1,3,1,128,2432]{3,2,4,1,0:T(2,128)(2,1)} %copy.49, s32[]{:T(128)} %constant.98.clone, s32[]{:T(128)} %constant.98.clone, s32[]{:T(128)S(6)} %select_n.49, s32[]{:T(128)} %constant.98.clone, s32[]{:T(128)} %constant.98.clone) | dynamic-update-slice | bytes 3735556 | tf_op jit(solution)/shard_map/while/body/eval_jaxpr/cond/branch_1_fun/dynamic_update_slice | solution.py:66
  4083.9 32.8 fusion.39
  4145.0 485.7 %conditional.2 = ((bf16[3,128,2432]{2,1,0:T(8,128)(2,1)}, bf16[1,3,8,128,2432]{3,2,4,1,0:T(8,128)(2,1)}, bf16[1,3,8,128,2432]{3,2,4,1,0:T(8,128)(2,1)})) conditional(s32[]{:T(128)} %convert_element_type.234, (bf16[3,128,2432]{2,1,0:T(8,128)(2,1)}, bf16[1,3,8,128,2432]{3,2,4,1,0:T(8,128)(2,1)}, bf16[1,3,8,128,2432]{3,2,4,1,0:T(8,128)(2,1)}) %tuple.71, ...), branch_computations={%region_1.1_spmd, %region_2.8_spmd} | conditional | flops 58521214976 | bytes 518665632 | solution.py:88
  4150.6 45.4 add_convert_fusion
  4277.1 95.9 %dynamic_update_slice.13 = bf16[1,3,8,128,2432]{3,2,4,1,0:T(8,128)(2,1)} dynamic-update-slice(bf16[1,3,8,128,2432]{3,2,4,1,0:T(8,128)(2,1)} %get-tuple-element.444, bf16[1,3,1,128,2432]{3,2,4,1,0:T(2,128)(2,1)} %copy.55, s32[]{:T(128)} %constant.98.clone, s32[]{:T(128)} %constant.98.clone, s32[]{:T(128)S(6)} %select_n.49, s32[]{:T(128)} %constant.98.clone, s32[]{:T(128)} %constant.98.clone) | dynamic-update-slice | bytes 3735556 | tf_op jit(solution)/shard_map/while/body/eval_jaxpr/cond/branch_1_fun/dynamic_update_slice | solution.py:65
  4440.0 95.9 %dynamic_update_slice.12 = bf16[1,3,8,128,2432]{3,2,4,1,0:T(8,128)(2,1)} dynamic-update-slice(bf16[1,3,8,128,2432]{3,2,4,1,0:T(8,128)(2,1)} %get-tuple-element.440, bf16[1,3,1,128,2432]{3,2,4,1,0:T(2,128)(2,1)} %copy.49, s32[]{:T(128)} %constant.98.clone, s32[]{:T(128)} %constant.98.clone, s32[]{:T(128)S(6)} %select_n.49, s32[]{:T(128)} %constant.98.clone, s32[]{:T(128)} %constant.98.clone) | dynamic-update-slice | bytes 3735556 | tf_op jit(solution)/shard_map/while/body/eval_jaxpr/cond/branch_1_fun/dynamic_update_slice | solution.py:66
  4597.7 32.8 fusion.39
  4659.1 485.8 %conditional.2 = ((bf16[3,128,2432]{2,1,0:T(8,128)(2,1)}, bf16[1,3,8,128,2432]{3,2,4,1,0:T(8,128)(2,1)}, bf16[1,3,8,128,2432]{3,2,4,1,0:T(8,128)(2,1)})) conditional(s32[]{:T(128)} %convert_element_type.234, (bf16[3,128,2432]{2,1,0:T(8,128)(2,1)}, bf16[1,3,8,128,2432]{3,2,4,1,0:T(8,128)(2,1)}, bf16[1,3,8,128,2432]{3,2,4,1,0:T(8,128)(2,1)}) %tuple.71, ...), branch_computations={%region_1.1_spmd, %region_2.8_spmd} | conditional | flops 58521214976 | bytes 518665632 | solution.py:88
  4664.8 45.4 add_convert_fusion
  4791.3 95.9 %dynamic_update_slice.13 = bf16[1,3,8,128,2432]{3,2,4,1,0:T(8,128)(2,1)} dynamic-update-slice(bf16[1,3,8,128,2432]{3,2,4,1,0:T(8,128)(2,1)} %get-tuple-element.444, bf16[1,3,1,128,2432]{3,2,4,1,0:T(2,128)(2,1)} %copy.55, s32[]{:T(128)} %constant.98.clone, s32[]{:T(128)} %constant.98.clone, s32[]{:T(128)S(6)} %select_n.49, s32[]{:T(128)} %constant.98.clone, s32[]{:T(128)} %constant.98.clone) | dynamic-update-slice | bytes 3735556 | tf_op jit(solution)/shard_map/while/body/eval_jaxpr/cond/branch_1_fun/dynamic_update_slice | solution.py:65
  4917.8 30.2 fusion.78
  4954.3 95.9 %dynamic_update_slice.12 = bf16[1,3,8,128,2432]{3,2,4,1,0:T(8,128)(2,1)} dynamic-update-slice(bf16[1,3,8,128,2432]{3,2,4,1,0:T(8,128)(2,1)} %get-tuple-element.440, bf16[1,3,1,128,2432]{3,2,4,1,0:T(2,128)(2,1)} %copy.49, s32[]{:T(128)} %constant.98.clone, s32[]{:T(128)} %constant.98.clone, s32[]{:T(128)S(6)} %select_n.49, s32[]{:T(128)} %constant.98.clone, s32[]{:T(128)} %constant.98.clone) | dynamic-update-slice | bytes 3735556 | tf_op jit(solution)/shard_map/while/body/eval_jaxpr/cond/branch_1_fun/dynamic_update_slice | solution.py:66
  5111.9 32.8 fusion.39
  5173.1 485.8 %conditional.2 = ((bf16[3,128,2432]{2,1,0:T(8,128)(2,1)}, bf16[1,3,8,128,2432]{3,2,4,1,0:T(8,128)(2,1)}, bf16[1,3,8,128,2432]{3,2,4,1,0:T(8,128)(2,1)})) conditional(s32[]{:T(128)} %convert_element_type.234, (bf16[3,128,2432]{2,1,0:T(8,128)(2,1)}, bf16[1,3,8,128,2432]{3,2,4,1,0:T(8,128)(2,1)}, bf16[1,3,8,128,2432]{3,2,4,1,0:T(8,128)(2,1)}) %tuple.71, ...), branch_computations={%region_1.1_spmd, %region_2.8_spmd} | conditional | flops 58521214976 | bytes 518665632 | solution.py:88
  5178.7 45.4 add_convert_fusion
  5304.9 95.9 %dynamic_update_slice.13 = bf16[1,3,8,128,2432]{3,2,4,1,0:T(8,128)(2,1)} dynamic-update-slice(bf16[1,3,8,128,2432]{3,2,4,1,0:T(8,128)(2,1)} %get-tuple-element.444, bf16[1,3,1,128,2432]{3,2,4,1,0:T(2,128)(2,1)} %copy.55, s32[]{:T(128)} %constant.98.clone, s32[]{:T(128)} %constant.98.clone, s32[]{:T(128)S(6)} %select_n.49, s32[]{:T(128)} %constant.98.clone, s32[]{:T(128)} %constant.98.clone) | dynamic-update-slice | bytes 3735556 | tf_op jit(solution)/shard_map/while/body/eval_jaxpr/cond/branch_1_fun/dynamic_update_slice | solution.py:65
  5467.9 95.9 %dynamic_update_slice.12 = bf16[1,3,8,128,2432]{3,2,4,1,0:T(8,128)(2,1)} dynamic-update-slice(bf16[1,3,8,128,2432]{3,2,4,1,0:T(8,128)(2,1)} %get-tuple-element.440, bf16[1,3,1,128,2432]{3,2,4,1,0:T(2,128)(2,1)} %copy.49, s32[]{:T(128)} %constant.98.clone, s32[]{:T(128)} %constant.98.clone, s32[]{:T(128)S(6)} %select_n.49, s32[]{:T(128)} %constant.98.clone, s32[]{:T(128)} %constant.98.clone) | dynamic-update-slice | bytes 3735556 | tf_op jit(solution)/shard_map/while/body/eval_jaxpr/cond/branch_1_fun/dynamic_update_slice | solution.py:66
  5625.6 32.8 fusion.39
  5722.5 209.4 %all-reduce.3.cloned.1.call-done = bf16[3,8,128,2432]{3,2,1,0:T(8,128)(2,1)} async-done(((bf16[3,8,128,2432]{3,2,1,0:T(8,128)(2,1)}), bf16[3,8,128,2432]{3,2,1,0:T(8,128)(2,1)}) %all-reduce.3.cloned.1.call-update) | async-done | bytes 14942224
  (399 shorter events, 1942.8 us)
Async XLA Ops:
  7.2 5924.8 %all-reduce.3.cloned.1.call-start = ((), (), s32[]{:S(2)}) async-start(), calls=%async_computation | async-start | bytes 29884416
  29.0 21.1 copy-start.5
  29.0 21.8 copy-start.6
  65.0 7.4 copy-start
  65.0 7.4 copy-start.4
  82.5 5.7 collective-permute-start
  85.5 2.8 copy-start.1
  91.2 18.1 collective-permute-start
  94.1 15.1 copy-start.1
  112.2 1460.4 %collective-permute-start = (bf16[3,128,2432]{2,1,0:T(8,128)(2,1)}, bf16[3,128,2432]{2,1,0:T(8,128)(2,1)S(1)}, u32[]{:S(2)}, u32[]{:S(2)}) collective-permute-start(bf16[3,128,2432]{2,1,0:T(8,128)(2,1)} %get-tuple-element.636), channel_id=1, source_target_pairs={{0,1},{1,2},{2,3},{4,5},{5,6},{6,7}} | collective-permute-start | bytes 5603336 | tf_op jit(solution)/shard_map/while/body/eval_jaxpr/ppermute | solution.py:92
  115.1 1457.5 %copy-start.1 = (bf16[1,17024]{1,0:T(2,128)(2,1)S(1)}, bf16[1,17024]{1,0:T(2,128)(2,1)}, u32[]{:S(2)}) copy-start(bf16[1,17024]{1,0:T(2,128)(2,1)} %get-tuple-element.736) | copy-start | bytes 102148 | tf_op jit(solution)/shard_map/while
  2018.9 9.0 copy-start.3
  2018.9 9.0 copy-start.2
  2060.9 25.4 collective-permute-start
  2063.9 22.5 copy-start.1
  2533.3 9.0 copy-start.3
  2533.3 9.0 copy-start.2
  2575.5 24.7 collective-permute-start
  2578.5 21.7 copy-start.1
  3047.0 9.0 copy-start.3
  3047.0 9.0 copy-start.2
  3089.0 25.3 collective-permute-start
  3092.0 22.3 copy-start.1
  3561.2 9.0 copy-start.3
  3561.3 9.0 copy-start.2
  3603.3 24.7 collective-permute-start
  3606.2 21.8 copy-start.1
  4074.9 9.0 copy-start.3
  4074.9 9.0 copy-start.2
  4117.2 24.7 collective-permute-start
  4120.1 21.7 copy-start.1
  4588.7 9.0 copy-start.3
  4588.7 9.0 copy-start.2
  4630.7 25.3 collective-permute-start
  4633.6 22.3 copy-start.1
  5102.9 9.0 copy-start.3
  5102.9 9.0 copy-start.2
  5144.9 24.7 collective-permute-start
  5147.9 21.8 copy-start.1
  5616.6 9.0 copy-start.3
  5616.6 9.0 copy-start.2
  5658.8 6.3 collective-permute-start
  5661.8 3.3 copy-start.1
  5700.2 21.1 copy-start.7
Sparse Core Ops, SparseCore 0:
  5679.1 252.7 all-reduce.2
where the time goes:
time: 6010 us; the launch traced here: 5940 us
  local copies, waits for them, and re-layouts  2350 us (39%)
  waiting for transfers between devices  1810 us (30%)
  matrix products  1100 us (18%)
  other arithmetic  640 us (11%)
    ppermute x11, waiting for transfers between devices, step_body(): recv_act = lax.ppermute(hidden, 'pp', send_pairs)  1600 us
    dynamic_update_slice x8, local copies, waits for them, and re-layouts, run_patch(): lax.dynamic_update_slice(k_buf, k_rot.reshape(1, batch_size, 1, patch_tok...  767 us
    dynamic_update_slice x8, local copies, waits for them, and re-layouts, run_patch(): lax.dynamic_update_slice(v_buf, v_fresh.reshape(1, batch_size, 1, patch_t...  767 us
    dot_general x8, matrix products, run_patch(): jnp.einsum('btd,de->bte', h_mod, w_one[layer_idx], preferred_element_type...  363 us
    dot_general x8, matrix products, run_patch(): jnp.einsum('bte,ed->btd', joined, w_two[layer_idx], preferred_element_typ...  262 us
    sub x8, matrix products, run_patch(): prob_bf = jax.nn.softmax(scores, axis=-1).astype(jnp.bfloat16)  241 us
    dot_general x8, matrix products, run_patch(): jnp.einsum('bhqk,bkhd->bqhd', prob_bf, val_all, preferred_element_type=jn...  215 us
    unnamed x2, waiting for transfers between devices  209 us
  transfers between devices with their start and end apart: 12, of which 11 were waited for; matrix products, arithmetic and copies ran while one was open for 2% of the time, Pallas kernels for 0%

commit v1 on v0

v1 whole, which is shorter than its diff:
```python
import functools
import math
import jax
import jax.numpy as jnp
from jax import lax
from jax.experimental import pallas as pl
from jax.experimental.pallas import tpu as pltpu
from jax.sharding import PartitionSpec as P

UNITS = 2
WEIGHT_SLOTS = 2
COL_BLOCK = 2432
LANES = 128


def rope_tables(pos_ids, head_dim):
    axis_zero = head_dim // 8
    axis_rest = (head_dim - axis_zero) // 2
    pieces = []
    for axis_idx, axis_dim in enumerate((axis_zero, axis_rest, head_dim - axis_zero - axis_rest)):
        axis_freqs = 1.0 / (10000.0 ** (jnp.arange(0, axis_dim, 2, dtype=jnp.float32) / axis_dim))
        pieces.append(pos_ids[..., axis_idx:axis_idx + 1].astype(jnp.float32) * axis_freqs)
    angles = jnp.concatenate(pieces, axis=-1)
    return jnp.cos(angles), jnp.sin(angles)


def col_blocks(width, body):
    full = width // COL_BLOCK

    def step(blk, carry):
        body(pl.multiple_of(blk * COL_BLOCK, LANES), COL_BLOCK)
        return carry

    lax.fori_loop(0, full, step, 0)
    if width % COL_BLOCK:
        body(full * COL_BLOCK, width % COL_BLOCK)


def stage_kernel(stages, units, head_dim,
                 x_in, mod, b_one, gains, cos_tab, sin_tab, ones_bd, b_two, w_one, w_two, k_prev, v_prev,
                 x_out, k_new, v_new, recv_x,
                 w_buf, k_buf, v_buf, x_buf, qkv, joined, acc, o_buf,
                 w_sem, kv_sem, x_sem, kv_out_sem, send_sem, local_sem, recv_sem, out_sem):
    stage = lax.axis_index('pp')
    samples, seq, width = x_in.shape
    rows = x_buf.shape[0]
    patch_tok = rows // units
    parts = seq // rows
    chunks = samples * parts
    slots = w_buf.shape[0]
    tiles_one = w_one.shape[1] // width
    tiles_two = w_two.shape[0] // width
    tiles = tiles_one + tiles_two
    last = stages - 1

    barrier = pltpu.get_barrier_semaphore()
    for hop in range(1, stages):
        pl.semaphore_signal(barrier, inc=1, device_id={'pp': lax.rem(stage + hop, stages)}, device_id_type=pl.DeviceIdType.MESH)
    pl.semaphore_wait(barrier, stages - 1)

    def tile_start(g):
        t = lax.rem(g, tiles)
        slot = lax.rem(g, slots)

        @pl.when(t < tiles_one)
        def _():
            pltpu.make_async_copy(w_one.at[:, pl.ds(pl.multiple_of(t * width, LANES), width)], w_buf.at[slot], w_sem.at[slot]).start()

        @pl.when(t >= tiles_one)
        def _():
            pltpu.make_async_copy(w_two.at[pl.ds(pl.multiple_of((t - tiles_one) * width, LANES), width), :], w_buf.at[slot], w_sem.at[slot]).start()

    def tile_wait(g):
        slot = lax.rem(g, slots)
        pltpu.make_async_copy(w_two.at[pl.ds(0, width), :], w_buf.at[slot], w_sem.at[slot]).wait()
        return slot

    def tile_done(g):
        @pl.when(g + slots < chunks * tiles)
        def _():
            tile_start(g + slots)

    for g0 in range(slots):
        tile_start(g0)

    def send_copy(c):
        s, part = lax.div(c, parts), lax.rem(c, parts)
        return pltpu.make_async_remote_copy(
            src_ref=o_buf, dst_ref=recv_x.at[s, pl.ds(pl.multiple_of(part * rows, LANES), rows), :],
            send_sem=send_sem, recv_sem=recv_sem.at[c],
            device_id={'pp': lax.rem(stage + 1, stages)}, device_id_type=pl.DeviceIdType.MESH)

    def out_copy(c):
        s, part = lax.div(c, parts), lax.rem(c, parts)
        return pltpu.make_async_remote_copy(
            src_ref=o_buf, dst_ref=x_out.at[s], send_sem=send_sem, recv_sem=out_sem.at[s],
            device_id={'pp': part}, device_id_type=pl.DeviceIdType.MESH)

    def local_copy(c):
        return pltpu.make_async_copy(o_buf, x_out.at[lax.div(c, parts)], local_sem)

    def out_start(c):
        part = lax.rem(c, parts)

        @pl.when(stage < last)
        def _():
            send_copy(c).start()

        @pl.when((stage == last) & (part < last))
        def _():
            out_copy(c).start()

        @pl.when((stage == last) & (part == last))
        def _():
            local_copy(c).start()

    def out_wait(c):
        part = lax.rem(c, parts)

        @pl.when(stage < last)
        def _():
            send_copy(c).wait_send()

        @pl.when((stage == last) & (part < last))
        def _():
            out_copy(c).wait_send()

        @pl.when((stage == last) & (part == last))
        def _():
            local_copy(c).wait()

    lane = lax.broadcasted_iota(jnp.int32, (patch_tok, LANES), 1)
    low_half = (lane < head_dim)
    low_bf = low_half.astype(jnp.float32).astype(jnp.bfloat16)
    high_bf = (1.0 - low_half.astype(jnp.float32)).astype(jnp.bfloat16)

    def chunk_body(c, carry):
        s, part = lax.div(c, parts), lax.rem(c, parts)
        row0 = pl.multiple_of(part * rows, LANES)
        base = c * tiles
        span = pl.ds(row0, rows)

        def prev_copies():
            return (pltpu.make_async_copy(k_prev.at[s], k_buf, kv_sem.at[0]),
                    pltpu.make_async_copy(v_prev.at[s], v_buf, kv_sem.at[1]))

        @pl.when(part == 0)
        def _():
            for cp in prev_copies():
                cp.start()

        @pl.when(stage == 0)
        def _():
            cp = pltpu.make_async_copy(x_in.at[s, span, :], x_buf, x_sem)
            cp.start()
            cp.wait()

        @pl.when(stage > 0)
        def _():
            send_copy(c).wait_recv()
            cp = pltpu.make_async_copy(recv_x.at[s, span, :], x_buf, x_sem)
            cp.start()
            cp.wait()

        norm_rows = 16

        def norm_step(r, carry):
            at = pl.ds(pl.multiple_of(r * norm_rows, norm_rows), norm_rows)
            act = x_buf[at, :].astype(jnp.float32)
            centered = act - jnp.mean(act, axis=-1, keepdims=True)
            normed = centered * lax.rsqrt(jnp.mean(centered * centered, axis=-1, keepdims=True) + 1e-6)
            joined[0, at, :] = (normed * (1.0 + mod[s, 1:2, :]) + mod[s, 0:1, :]).astype(jnp.bfloat16)
            return carry

        lax.fori_loop(0, rows // norm_rows, norm_step, 0, unroll=2)

        def proj(slot, j, off, size):
            cols = pl.ds(off, size)
            out = jnp.dot(joined[0], w_buf[slot, :, cols], preferred_element_type=jnp.float32)
            return (out + b_one[j, :, cols]).astype(jnp.bfloat16)

        def head_tile(j, carry):
            slot = tile_wait(base + j)
            even = (lax.broadcasted_iota(jnp.int32, (rows, LANES), 1) & 1) == 0

            def body(off, size):
                raw = proj(slot, j, off, size).astype(jnp.float32)
                cos_v = cos_tab[span, :]
                sin_v = sin_tab[span, :]
                for lo in range(0, size, 2 * LANES):
                    wide = min(2 * LANES, size - lo)
                    sub = raw[:, lo:lo + wide]
                    sq = sub * sub
                    ones = ones_bd[:wide, :wide]
                    sq0 = sq.astype(jnp.bfloat16)
                    rem1 = sq - sq0.astype(jnp.float32)
                    sq1 = rem1.astype(jnp.bfloat16)
                    sq2 = (rem1 - sq1.astype(jnp.float32)).astype(jnp.bfloat16)
                    total = jnp.dot(sq0, ones, preferred_element_type=jnp.float32)
                    total += jnp.dot(sq1, ones, preferred_element_type=jnp.float32)
                    total += jnp.dot(sq2, ones, preferred_element_type=jnp.float32)
                    inv = lax.rsqrt(total * (1.0 / head_dim) + 1e-6)
                    for l2 in range(0, wide, LANES):
                        one = sub[:, l2:l2 + LANES] * inv[:, l2:l2 + LANES] * gains[j]
                        swapped = jnp.where(even, pltpu.roll(one, LANES - 1, 1), pltpu.roll(one, 1, 1))
                        rot = one * cos_v + swapped * sin_v
                        qkv[j, :, pl.ds(off + lo + l2, LANES)] = rot.astype(jnp.bfloat16)

            col_blocks(width, body)
            tile_done(base + j)
            return carry

        lax.fori_loop(0, 2, head_tile, 0)

        slot_v = tile_wait(base + 2)

        def value_body(off, size):
            qkv[2, :, pl.ds(off, size)] = proj(slot_v, 2, off, size)

        col_blocks(width, value_body)
        tile_done(base + 2)

        def fresh_copies():
            return (pltpu.make_async_copy(qkv.at[1], k_new.at[s, span, :], kv_out_sem.at[0]),
                    pltpu.make_async_copy(qkv.at[2], v_new.at[s, span, :], kv_out_sem.at[1]))

        for cp in fresh_copies():
            cp.start()

        def mlp_tile(j, carry):
            slot = tile_wait(base + j)

            def body(off, size):
                pre = proj(slot, j, off, size).astype(jnp.float32)
                joined[j - 2, :, pl.ds(off, size)] = jax.nn.gelu(pre, approximate=True).astype(jnp.bfloat16)

            col_blocks(width, body)
            tile_done(base + j)
            return carry

        lax.fori_loop(3, tiles_one, mlp_tile, 0)

        @pl.when(part == 0)
        def _():
            for cp in prev_copies():
                cp.wait()

        def unit_step(u, carry):
            q_rows = pl.ds(pl.multiple_of(u * patch_tok, LANES), patch_tok)
            key_rows = pl.ds(pl.multiple_of(row0 + u * patch_tok, LANES), patch_tok)
            k_buf[key_rows, :] = qkv[1, q_rows, :]
            v_buf[key_rows, :] = qkv[2, q_rows, :]

            def pair(off):
                cols = pl.ds(off, LANES)
                q2 = qkv[0, q_rows, cols]
                both = jnp.concatenate([q2 * low_bf, q2 * high_bf], axis=0)
                scores = lax.dot_general(both, k_buf[:, cols], (((1,), (1,)), ((), ())), preferred_element_type=jnp.float32)
                top = jnp.max(scores, axis=-1, keepdims=True)
                ex = jnp.exp(scores - top)
                prob = (ex * (1.0 / jnp.sum(ex, axis=-1, keepdims=True))).astype(jnp.bfloat16)
                mixed = jnp.dot(prob, v_buf[:, cols], preferred_element_type=jnp.float32)
                joined[0, q_rows, cols] = jnp.where(low_half, mixed[:patch_tok], mixed[patch_tok:]).astype(jnp.bfloat16)

            pairs = width // LANES
            group = 3

            def pair_step(i, carry):
                for k in range(group):
                    pair(pl.multiple_of((i * group + k) * LANES, LANES))
                return carry

            lax.fori_loop(0, pairs // group, pair_step, 0)
            for k in range(pairs - pairs % group, pairs):
                pair(k * LANES)
            return carry

        lax.fori_loop(0, units, unit_step, 0)

        def two_tile(j, carry):
            slot = tile_wait(base + tiles_one + j)

            def body(off, size):
                cols = pl.ds(off, size)
                part_sum = jnp.dot(joined[j], w_buf[slot, :, cols], preferred_element_type=jnp.float32)
                acc[:, cols] = acc[:, cols] + part_sum

            col_blocks(width, body)
            tile_done(base + tiles_one + j)
            return carry

        acc[...] = jnp.zeros_like(acc)
        lax.fori_loop(0, tiles_two, two_tile, 0)

        for cp in fresh_copies():
            cp.wait()

        @pl.when(c > 0)
        def _():
            out_wait(c - 1)

        def res_step(r, carry):
            at = pl.ds(pl.multiple_of(r * norm_rows, norm_rows), norm_rows)
            block_out = acc[at, :] + b_two[...]
            o_buf[at, :] = (x_buf[at, :].astype(jnp.float32) + mod[s, 2:3, :] * block_out).astype(jnp.bfloat16)
            return carry

        lax.fori_loop(0, rows // norm_rows, res_step, 0, unroll=2)
        out_start(c)
        return carry

    lax.fori_loop(0, chunks, chunk_body, 0)
    out_wait(chunks - 1)

    @pl.when(stage < last)
    def _():
        for s in range(samples):
            out_copy(s * parts).wait_recv()


def solution(mesh):
    stages = mesh.shape['pp']

    def stage_program(x_in, cond_vec, pos_ids, w_mod, b_mod, w_one, b_one, qk_scale, w_two, b_two, k_prev, v_prev):
        samples, patches, patch_tok, width = x_in.shape
        head_dim = qk_scale.shape[-1]
        seq = patches * patch_tok
        rows = UNITS * patch_tok
        chunks = samples * seq // rows
        tiles_one = w_one.shape[2] // width
        tiles_two = w_two.shape[1] // width
        cond_act = jax.nn.silu(cond_vec.astype(jnp.float32)).astype(jnp.bfloat16)
        mod = jnp.dot(cond_act, w_mod[0], preferred_element_type=jnp.float32) + b_mod.astype(jnp.float32)
        mod = mod.reshape(samples, 3, width)
        cos_tab, sin_tab = rope_tables(pos_ids.reshape(seq, 3), head_dim)
        heads_in_lane = LANES // head_dim
        cos_tab = jnp.tile(jnp.repeat(cos_tab, 2, axis=-1), (1, heads_in_lane))
        sin_tab = jnp.stack([-sin_tab, sin_tab], axis=-1).reshape(seq, head_dim)
        sin_tab = jnp.tile(sin_tab, (1, heads_in_lane))
        scale = jnp.array([1.0 / math.sqrt(head_dim), 1.0], jnp.float32)
        gains = jnp.tile(qk_scale[0].astype(jnp.float32) * scale[:, None], (1, heads_in_lane)).reshape(2, 1, LANES)
        group = jnp.arange(2 * LANES) // head_dim
        ones_bd = (group[:, None] == group[None, :]).astype(jnp.bfloat16)
        vmem = pl.BlockSpec(memory_space=pltpu.VMEM)
        hbm = pl.BlockSpec(memory_space=pl.ANY)
        act = jax.ShapeDtypeStruct((samples, seq, width), jnp.bfloat16)
        x_part = jax.ShapeDtypeStruct((samples, seq // stages, width), jnp.bfloat16)
        bf = jnp.bfloat16
        x_out, k_new, v_new, _ = pl.pallas_call(
            functools.partial(stage_kernel, stages, UNITS, head_dim),
            out_shape=(x_part, act, act, act),
            in_specs=[hbm] + [vmem] * 7 + [hbm] * 4,
            out_specs=(hbm, hbm, hbm, hbm),
            scratch_shapes=[
                pltpu.VMEM((WEIGHT_SLOTS, width, width), bf),
                pltpu.VMEM((seq, width), bf), pltpu.VMEM((seq, width), bf),
                pltpu.VMEM((rows, width), bf),
                pltpu.VMEM((3, rows, width), bf),
                pltpu.VMEM((tiles_two, rows, width), bf),
                pltpu.VMEM((rows, width), jnp.float32),
                pltpu.VMEM((rows, width), bf),
                pltpu.SemaphoreType.DMA((WEIGHT_SLOTS,)),
                pltpu.SemaphoreType.DMA((2,)),
                pltpu.SemaphoreType.DMA,
                pltpu.SemaphoreType.DMA((2,)),
                pltpu.SemaphoreType.DMA,
                pltpu.SemaphoreType.DMA,
                pltpu.SemaphoreType.DMA((chunks,)),
                pltpu.SemaphoreType.DMA((samples,)),
            ],
            compiler_params=pltpu.CompilerParams(collective_id=0, has_side_effects=True, vmem_limit_bytes=67043328),
            name='stage_kernel',
        )(x_in.reshape(samples, seq, width), mod, b_one.astype(jnp.float32).reshape(tiles_one, 1, width), gains, cos_tab, sin_tab, ones_bd,
          b_two.astype(jnp.float32), w_one[0], w_two[0], k_prev.reshape(samples, seq, width), v_prev.reshape(samples, seq, width))
        x_out = x_out.reshape(samples, patches // stages, patch_tok, width)
        return x_out, k_new.reshape(k_prev.shape), v_new.reshape(v_prev.shape)

    return jax.shard_map(
        stage_program, mesh=mesh,
        in_specs=(P('dp'), P('dp'), P(), P('pp'), P('pp'), P('pp'), P('pp'), P('pp'), P('pp'), P('pp'), P('pp', 'dp'), P('pp', 'dp')),
        out_specs=(P('dp', 'pp'), P('pp', 'dp'), P('pp', 'dp')),
        check_vma=False)
```

time: 6010 us -> 1330 us (0.22); the launches traced: 5940 us -> 1330 us
  local copies, waits for them, and re-layouts: 2350 us -> 29.2 us
  waiting for transfers between devices: 1810 us -> 0 us
  Pallas kernels: 0 us -> 1270 us
  matrix products: 1100 us -> 15.8 us
  other arithmetic: 640 us -> 6.34 us
    ppermute x11 -> x0, waiting for transfers between devices: 1600 us -> none  [step_body(): recv_act = lax.ppermute(hidden, 'pp', send_pairs)]
    dynamic_update_slice x16 -> x0, local copies, waits for them, and re-layouts: 1530 us -> none  [the longest x8 767 us: run_patch(): lax.dynamic_update_slice(k_buf, k_rot.reshape(1, batch_size, 1, patch_tok...]
    pallas_call x0 -> x1, Pallas kernels: none -> 1270 us  [stage_program(): pl.pallas_call(functools.partial(stage_kernel, stages, UNITS, head_dim),...]
    dot_general x25 -> x1, matrix products: 855 us -> 15.8 us  [stage_program(): jnp.dot(cond_act, w_mod[0], preferred_element_type=jnp.float32)]
    squeeze x16 -> x0, local copies, waits for them, and re-layouts: 369 us -> none  [the longest x8 185 us: run_patch(): k_buf[layer_idx].reshape(batch_size, seq_len, head_count, head_dim)]
    sub x8 -> x0, matrix products: 241 us -> none  [run_patch(): prob_bf = jax.nn.softmax(scores, axis=-1).astype(jnp.bfloat16)]
    unnamed x2 -> x0, waiting for transfers between devices: 209 us -> none
    another operation x24 -> x1, other arithmetic: 198 us -> 0.02 us  [stage_program(): sin_tab = jnp.stack([-sin_tab, sin_tab], axis=-1).reshape(seq, head_dim)]
  transfers between devices with their start and end apart: 12 -> 0, of which waited for: 11 -> 0; matrix products, arithmetic and copies ran while one was open for 2% -> 0% of each run, Pallas kernels for 0% -> 0%
where the time goes in v1:
time: 1330 us
  Pallas kernels  1270 us (95%)
  local copies, waits for them, and re-layouts  29.2 us (2%)
  matrix products  15.8 us (1%)
    pallas_call x1, Pallas kernels, stage_program(): pl.pallas_call(functools.partial(stage_kernel, stages, UNITS, head_dim),...  1270 us

profile of v1, /device:TPU:7, one launch (start us, length us, event | category | flops | bytes accessed | tf_op | source)
XLA Modules:
  0.0 1325.3 jit_solution(6027463903605614319)
XLA Ops:
  0.7 0.7 convert_multiply_fusion.1
  1.4 0.6 tile.29.gains
  2.1 1.3 convert_element_type.41.b_two
  3.4 0.7 copy.23
  4.1 0.1 fusion.12
  4.2 0.8 convert_reduce_fusion
  5.0 1.6 convert.3.b_one
  6.6 15.8 %fusion.2 = f32[3,7296]{1,0:T(4,128)S(1)} fusion(bf16[1,2432,7296]{2,1,0:T(8,128)(2,1)} %param.16, f32[7296]{0:T(1024)S(1)} %convert_reduce_fusion, bf16[3,2432]{1,0:T(4,128)(2,1)} %param.14), kind=kOutput, calls=%fused_computation.2 | convolution fusion | flops 106528896 | bytes 35619072 | tf_op jit(solution)/shard_map/dot_general | solution.py:333
  22.4 0.7 reshape.280.mod
  23.1 0.8 compare_convert_fusion.ones_bd
  23.9 0.1 fusion.10
  23.9 0.4 maximum_cosine_fusion
  24.4 0.5 fusion.14
  24.9 0.2 copy.18
  25.1 0.2 tile.33
  25.3 0.1 broadcast_in_dim.2
  25.4 0.2 tile.30
  25.6 1.0 copy.19.cos_tab
  26.7 1.0 copy.20.sin_tab
  27.7 1273.3 %stage_kernel.1 = (bf16[3,256,2432]{2,1,0:T(8,128)(2,1)}, bf16[3,1024,2432]{2,1,0:T(8,128)(2,1)}, bf16[3,1024,2432]{2,1,0:T(8,128)(2,1)}, bf16[3,1024,2432]{2,1,0:T(8,128)(2,1)}) custom-call(bf16[3,1024,2432]{2,1,0:T(8,128)(2,1)} %bitcast.44, f32[3,3,2432]{2,1,0:T(4,128)} %reshape.280.mod, f32[7,1,2432]{2,1,0:T(1,128)} %convert.3.b_one, ...), custom_call_target="tpu_custom_call" | custom-call | tf_op jit(solution)/shard_map/stage_kernel/pallas_call | solution.py:349
  1301.0 0.0 slice-start
  1301.0 4.3 copy.27
  1305.3 0.0 slice-start.1
  1305.3 0.0 slice-start.2
  1305.3 0.0 slice-start.3
  1305.3 13.1 copy.28
  1318.5 0.0 slice-done
  1318.5 0.0 slice-done.1
  1318.5 0.0 slice-done.2
  1318.5 1.3 slice-done.3
  1319.8 5.6 copy.29
  (9 shorter events, 0.1 us)
Async XLA Ops:
  1301.0 17.5 %slice-start = ((s8[14942208]{0:T(1024)(128)(4,1)}), s8[2359296]{0:T(1024)(128)(4,1)S(1)}, s32[]{:S(2)}) async-start(s8[14942208]{0:T(1024)(128)(4,1)} %bitcast.40), calls=%async_computation | async-start | bytes 4718592
  1305.3 13.1 slice-start.1
  1305.3 13.2 slice-start.2
  1305.3 14.5 %slice-start.3 = ((s8[14942208]{0:T(1024)(128)(4,1)}), s8[4194304]{0:T(1024)(128)(4,1)S(1)}, s32[]{:S(2)}) async-start(s8[14942208]{0:T(1024)(128)(4,1)} %bitcast.40), calls=%async_computation.3 | async-start | bytes 8388608

commit v2 on v1

v2 whole, which is shorter than its diff:
```python
import functools
import math
import jax
import jax.numpy as jnp
from jax import lax
from jax.experimental import pallas as pl
from jax.experimental.pallas import tpu as pltpu
from jax.sharding import PartitionSpec as P

UNITS = 2
WEIGHT_SLOTS = 4
LANES = 128
SOFT_ROWS = 16


def rope_tables(pos_ids, head_dim):
    axis_zero = head_dim // 8
    axis_rest = (head_dim - axis_zero) // 2
    pieces = []
    for axis_idx, axis_dim in enumerate((axis_zero, axis_rest, head_dim - axis_zero - axis_rest)):
        axis_freqs = 1.0 / (10000.0 ** (jnp.arange(0, axis_dim, 2, dtype=jnp.float32) / axis_dim))
        pieces.append(pos_ids[..., axis_idx:axis_idx + 1].astype(jnp.float32) * axis_freqs)
    angles = jnp.concatenate(pieces, axis=-1)
    return jnp.cos(angles), jnp.sin(angles)


def tile_halves(width):
    second = max(width // (4 * LANES) // 2, 1) * 4 * LANES if width >= 8 * LANES else LANES
    return ((0, width - second), (width - second, second))


def stage_kernel(stages, units, head_dim,
                 x_in, mod, b_one, gains, cos_tab, sin_tab, ones_bd, b_two, w_one, w_two, k_prev, v_prev,
                 x_out, k_new, v_new,
                 w_buf, k_buf, v_buf, x_buf, qkv, joined, acc, o_buf, score0, score1, prob0, prob1,
                 w_sem, kv_sem, x_sem, kv_out_sem, send_sem, local_sem, recv_sem, out_sem, free_sem):
    stage = lax.axis_index('pp')
    samples, seq, width = x_in.shape
    rows = x_buf.shape[1]
    patch_tok = rows // units
    parts = seq // rows
    chunks = samples * parts
    slots = w_buf.shape[0]
    tiles_one = w_one.shape[1] // width
    tiles_two = w_two.shape[0] // width
    tiles = tiles_one + tiles_two
    last = stages - 1

    barrier = pltpu.get_barrier_semaphore()
    for hop in range(1, stages):
        pl.semaphore_signal(barrier, inc=1, device_id={'pp': lax.rem(stage + hop, stages)}, device_id_type=pl.DeviceIdType.MESH)
    pl.semaphore_wait(barrier, stages - 1)

    halves = tile_halves(width)

    def half_start(g, half):
        off, size = halves[half]
        t = lax.rem(lax.div(g, 2), tiles)
        slot = lax.rem(g, slots)
        dst = w_buf.at[slot, :, pl.ds(0, size)]

        @pl.when(t < tiles_one)
        def _():
            pltpu.make_async_copy(w_one.at[:, pl.ds(pl.multiple_of(t * width + off, LANES), size)], dst, w_sem.at[slot]).start()

        @pl.when(t >= tiles_one)
        def _():
            pltpu.make_async_copy(w_two.at[pl.ds(pl.multiple_of((t - tiles_one) * width, LANES), width), pl.ds(off, size)], dst, w_sem.at[slot]).start()

    def run_tile(tile, body):
        for half, (off, size) in enumerate(halves):
            g = 2 * tile + half
            slot = lax.rem(g, slots)
            weights = w_buf.at[slot, :, pl.ds(0, size)]
            pltpu.make_async_copy(w_two.at[pl.ds(0, width), pl.ds(off, size)], weights, w_sem.at[slot]).wait()
            body(weights, off, size)

            @pl.when(g + slots < 2 * chunks * tiles)
            def _():
                half_start(g + slots, (half + slots) % 2)

    for g0 in range(slots):
        half_start(g0, g0 % 2)

    def send_copy(c):
        return pltpu.make_async_remote_copy(
            src_ref=o_buf, dst_ref=x_buf.at[lax.rem(c, 2)],
            send_sem=send_sem, recv_sem=recv_sem.at[c],
            device_id={'pp': lax.rem(stage + 1, stages)}, device_id_type=pl.DeviceIdType.MESH)

    def out_copy(c):
        s, part = lax.div(c, parts), lax.rem(c, parts)
        return pltpu.make_async_remote_copy(
            src_ref=o_buf, dst_ref=x_out.at[s], send_sem=send_sem, recv_sem=out_sem.at[s],
            device_id={'pp': part}, device_id_type=pl.DeviceIdType.MESH)

    def local_copy(c):
        return pltpu.make_async_copy(o_buf, x_out.at[lax.div(c, parts)], local_sem)

    def out_start(c):
        part = lax.rem(c, parts)

        @pl.when(stage < last)
        def _():
            @pl.when(c >= 2)
            def _():
                pl.semaphore_wait(free_sem, 1)

            send_copy(c).start()

        @pl.when((stage == last) & (part < last))
        def _():
            out_copy(c).start()

        @pl.when((stage == last) & (part == last))
        def _():
            local_copy(c).start()

    def out_wait(c):
        part = lax.rem(c, parts)

        @pl.when(stage < last)
        def _():
            send_copy(c).wait_send()

        @pl.when((stage == last) & (part < last))
        def _():
            out_copy(c).wait_send()

        @pl.when((stage == last) & (part == last))
        def _():
            local_copy(c).wait()

    def in_copy(c):
        s, part = lax.div(c, parts), lax.rem(c, parts)
        slot = lax.rem(c, 2)
        return pltpu.make_async_copy(x_in.at[s, pl.ds(pl.multiple_of(part * rows, LANES), rows), :], x_buf.at[slot], x_sem.at[slot])

    @pl.when(stage == 0)
    def _():
        in_copy(0).start()

    lane = lax.broadcasted_iota(jnp.int32, (patch_tok, LANES), 1)
    low_half = (lane < head_dim)
    low_bf = low_half.astype(jnp.float32).astype(jnp.bfloat16)
    high_bf = (1.0 - low_half.astype(jnp.float32)).astype(jnp.bfloat16)

    def chunk_body(c, carry):
        s, part = lax.div(c, parts), lax.rem(c, parts)
        row0 = pl.multiple_of(part * rows, LANES)
        base = c * tiles
        span = pl.ds(row0, rows)

        def prev_copies():
            return (pltpu.make_async_copy(k_prev.at[s], k_buf, kv_sem.at[0]),
                    pltpu.make_async_copy(v_prev.at[s], v_buf, kv_sem.at[1]))

        @pl.when(part == 0)
        def _():
            for cp in prev_copies():
                cp.start()

        @pl.when(stage == 0)
        def _():
            in_copy(c).wait()

            @pl.when(c + 1 < chunks)
            def _():
                in_copy(c + 1).start()

        @pl.when(stage > 0)
        def _():
            send_copy(c).wait_recv()

        x_now = x_buf.at[lax.rem(c, 2)]
        norm_rows = 16

        def norm_step(r, carry):
            at = pl.ds(pl.multiple_of(r * norm_rows, norm_rows), norm_rows)
            act = x_now[at, :].astype(jnp.float32)
            centered = act - jnp.mean(act, axis=-1, keepdims=True)
            normed = centered * lax.rsqrt(jnp.mean(centered * centered, axis=-1, keepdims=True) + 1e-6)
            joined[0, at, :] = (normed * (1.0 + mod[s, 1:2, :]) + mod[s, 0:1, :]).astype(jnp.bfloat16)
            return carry

        lax.fori_loop(0, rows // norm_rows, norm_step, 0, unroll=4)

        def proj(weights, j, off, size):
            out = jnp.dot(joined[0], weights[...], preferred_element_type=jnp.float32)
            return (out + b_one[j, :, pl.ds(off, size)]).astype(jnp.bfloat16)

        def head_tile(j, carry):
            even = (lax.broadcasted_iota(jnp.int32, (rows, LANES), 1) & 1) == 0

            def rotate(raw, off):
                cos_v = cos_tab[span, :]
                sin_v = sin_tab[span, :]
                size = raw.shape[1]
                for lo in range(0, size, 2 * LANES):
                    wide = min(2 * LANES, size - lo)
                    sub = raw[:, lo:lo + wide].astype(jnp.float32)
                    sq = sub * sub
                    ones = ones_bd[:wide, :wide]
                    sq0 = sq.astype(jnp.bfloat16)
                    sq1 = (sq - sq0.astype(jnp.float32)).astype(jnp.bfloat16)
                    total = jnp.dot(sq0, ones, preferred_element_type=jnp.float32)
                    total += jnp.dot(sq1, ones, preferred_element_type=jnp.float32)
                    inv = lax.rsqrt(total * (1.0 / head_dim) + 1e-6)
                    for l2 in range(0, wide, LANES):
                        one = sub[:, l2:l2 + LANES] * inv[:, l2:l2 + LANES] * gains[j]
                        swapped = jnp.where(even, pltpu.roll(one, LANES - 1, 1), pltpu.roll(one, 1, 1))
                        rot = one * cos_v + swapped * sin_v
                        qkv[j, :, off + lo + l2:off + lo + l2 + LANES] = rot.astype(jnp.bfloat16)

            def body(weights, off, size):
                waiting = None
                for lo in range(0, size, 4 * LANES):
                    wide = min(4 * LANES, size - lo)
                    fresh = (proj(weights.at[:, pl.ds(lo, wide)], j, off + lo, wide), off + lo)
                    if waiting is not None:
                        rotate(*waiting)
                    waiting = fresh
                rotate(*waiting)

            run_tile(base + j, body)
            return carry

        lax.fori_loop(0, 2, head_tile, 0)

        def value_body(weights, off, size):
            qkv[2, :, pl.ds(off, size)] = proj(weights, 2, off, size)

        run_tile(base + 2, value_body)

        def fresh_copies():
            return (pltpu.make_async_copy(qkv.at[1], k_new.at[s, span, :], kv_out_sem.at[0]),
                    pltpu.make_async_copy(qkv.at[2], v_new.at[s, span, :], kv_out_sem.at[1]))

        for cp in fresh_copies():
            cp.start()

        def mlp_tile(j, carry):
            def body(weights, off, size):
                pre = proj(weights, j, off, size).astype(jnp.float32)
                joined[j - 2, :, pl.ds(off, size)] = jax.nn.gelu(pre, approximate=True).astype(jnp.bfloat16)

            run_tile(base + j, body)
            return carry

        lax.fori_loop(3, tiles_one, mlp_tile, 0)

        @pl.when(part == 0)
        def _():
            for cp in prev_copies():
                cp.wait()

        def unit_step(u, carry):
            q_rows = pl.ds(pl.multiple_of(u * patch_tok, LANES), patch_tok)
            key_rows = pl.ds(pl.multiple_of(row0 + u * patch_tok, LANES), patch_tok)
            k_buf[key_rows, :] = qkv[1, q_rows, :]
            v_buf[key_rows, :] = qkv[2, q_rows, :]

            pairs = width // LANES
            quads = -(-pairs // 2)
            two_rows = 2 * patch_tok

            def first_pair(quad):
                return min(2 * quad, pairs - 2)

            def score(quad, which, dst):
                cols = pl.ds((first_pair(quad) + which) * LANES, LANES)
                q2 = qkv[0, q_rows, cols]
                both = jnp.concatenate([q2 * low_bf, q2 * high_bf], axis=0)
                dst[...] = lax.dot_general(both, k_buf[:, cols], (((1,), (1,)), ((), ())), preferred_element_type=jnp.float32)

            def soften(which, src, dst):
                for r in range(0, two_rows, SOFT_ROWS):
                    sc = src[r:r + SOFT_ROWS, :]
                    ex = jnp.exp(sc - jnp.max(sc, axis=-1, keepdims=True))
                    at = which * two_rows + r
                    dst[at:at + SOFT_ROWS, :] = (ex * (1.0 / jnp.sum(ex, axis=-1, keepdims=True))).astype(jnp.bfloat16)

            def mix(quad, src):
                cols = pl.ds(first_pair(quad) * LANES, 2 * LANES)
                mixed = jnp.dot(src[...], v_buf[:, cols], preferred_element_type=jnp.float32)
                t = patch_tok
                out = jnp.concatenate([jnp.where(low_half, mixed[:t, :LANES], mixed[t:2 * t, :LANES]),
                                       jnp.where(low_half, mixed[2 * t:3 * t, LANES:], mixed[3 * t:, LANES:])], axis=1)
                joined[0, q_rows, cols] = out.astype(jnp.bfloat16)

            def quad_step(quad, before, now):
                if before is not None:
                    mix(quad - 1, before)
                for which, buf in enumerate((score0, score1)):
                    soften(which, buf, now)
                    if quad + 1 < quads:
                        score(quad + 1, which, buf)

            score(0, 0, score0)
            score(0, 1, score1)
            quad_step(0, None, prob0)

            probs = (prob0, prob1)
            for quad in range(1, quads):
                quad_step(quad, probs[1 - quad % 2], probs[quad % 2])
            mix(quads - 1, probs[(quads - 1) % 2])
            return carry

        lax.fori_loop(0, units, unit_step, 0)

        def two_tile(j, carry):
            def body(weights, off, size):
                cols = pl.ds(off, size)
                acc[:, cols] = acc[:, cols] + jnp.dot(joined[j], weights[...], preferred_element_type=jnp.float32)

            run_tile(base + tiles_one + j, body)
            return carry

        acc[...] = jnp.zeros_like(acc)
        lax.fori_loop(0, tiles_two, two_tile, 0)

        for cp in fresh_copies():
            cp.wait()

        @pl.when(c > 0)
        def _():
            out_wait(c - 1)

        def res_step(r, carry):
            at = pl.ds(pl.multiple_of(r * norm_rows, norm_rows), norm_rows)
            block_out = acc[at, :] + b_two[...]
            o_buf[at, :] = (x_now[at, :].astype(jnp.float32) + mod[s, 2:3, :] * block_out).astype(jnp.bfloat16)
            return carry

        lax.fori_loop(0, rows // norm_rows, res_step, 0, unroll=2)
        @pl.when((stage > 0) & (c + 2 < chunks))
        def _():
            pl.semaphore_signal(free_sem, inc=1, device_id={'pp': lax.rem(stage + stages - 1, stages)}, device_id_type=pl.DeviceIdType.MESH)

        out_start(c)
        return carry

    lax.fori_loop(0, chunks, chunk_body, 0)
    out_wait(chunks - 1)

    @pl.when(stage < last)
    def _():
        for s in range(samples):
            out_copy(s * parts).wait_recv()


def solution(mesh):
    stages = mesh.shape['pp']

    def stage_program(x_in, cond_vec, pos_ids, w_mod, b_mod, w_one, b_one, qk_scale, w_two, b_two, k_prev, v_prev):
        samples, patches, patch_tok, width = x_in.shape
        head_dim = qk_scale.shape[-1]
        seq = patches * patch_tok
        rows = UNITS * patch_tok
        chunks = samples * seq // rows
        tiles_one = w_one.shape[2] // width
        tiles_two = w_two.shape[1] // width
        cond_act = jax.nn.silu(cond_vec.astype(jnp.float32)).astype(jnp.bfloat16)
        mod = jnp.dot(cond_act, w_mod[0], preferred_element_type=jnp.float32) + b_mod.astype(jnp.float32)
        mod = mod.reshape(samples, 3, width)
        cos_tab, sin_tab = rope_tables(pos_ids.reshape(seq, 3), head_dim)
        heads_in_lane = LANES // head_dim
        cos_tab = jnp.tile(jnp.repeat(cos_tab, 2, axis=-1), (1, heads_in_lane))
        sin_tab = jnp.stack([-sin_tab, sin_tab], axis=-1).reshape(seq, head_dim)
        sin_tab = jnp.tile(sin_tab, (1, heads_in_lane))
        scale = jnp.array([1.0 / math.sqrt(head_dim), 1.0], jnp.float32)
        gains = jnp.tile(qk_scale[0].astype(jnp.float32) * scale[:, None], (1, heads_in_lane)).reshape(2, 1, LANES)
        group = jnp.arange(2 * LANES) // head_dim
        ones_bd = (group[:, None] == group[None, :]).astype(jnp.bfloat16)
        vmem = pl.BlockSpec(memory_space=pltpu.VMEM)
        hbm = pl.BlockSpec(memory_space=pl.ANY)
        act = jax.ShapeDtypeStruct((samples, seq, width), jnp.bfloat16)
        x_part = jax.ShapeDtypeStruct((samples, seq // stages, width), jnp.bfloat16)
        bf = jnp.bfloat16
        x_out, k_new, v_new = pl.pallas_call(
            functools.partial(stage_kernel, stages, UNITS, head_dim),
            out_shape=(x_part, act, act),
            in_specs=[hbm] + [vmem] * 7 + [hbm] * 4,
            out_specs=(hbm, hbm, hbm),
            scratch_shapes=[
                pltpu.VMEM((WEIGHT_SLOTS, width, tile_halves(width)[0][1]), bf),
                pltpu.VMEM((seq, width), bf), pltpu.VMEM((seq, width), bf),
                pltpu.VMEM((2, rows, width), bf),
                pltpu.VMEM((3, rows, width), bf),
                pltpu.VMEM((tiles_two, rows, width), bf),
                pltpu.VMEM((rows, width), jnp.float32),
                pltpu.VMEM((rows, width), bf),
                pltpu.VMEM((2 * patch_tok, seq), jnp.float32), pltpu.VMEM((2 * patch_tok, seq), jnp.float32),
                pltpu.VMEM((4 * patch_tok, seq), bf), pltpu.VMEM((4 * patch_tok, seq), bf),
                pltpu.SemaphoreType.DMA((WEIGHT_SLOTS,)),
                pltpu.SemaphoreType.DMA((2,)),
                pltpu.SemaphoreType.DMA((2,)),
                pltpu.SemaphoreType.DMA((2,)),
                pltpu.SemaphoreType.DMA,
                pltpu.SemaphoreType.DMA,
                pltpu.SemaphoreType.DMA((chunks,)),
                pltpu.SemaphoreType.DMA((samples,)),
                pltpu.SemaphoreType.REGULAR,
            ],
            compiler_params=pltpu.CompilerParams(collective_id=0, has_side_effects=True, vmem_limit_bytes=67043328),
            name='stage_kernel',
        )(x_in.reshape(samples, seq, width), mod, b_one.astype(jnp.float32).reshape(tiles_one, 1, width), gains, cos_tab, sin_tab, ones_bd,
          b_two.astype(jnp.float32), w_one[0], w_two[0], k_prev.reshape(samples, seq, width), v_prev.reshape(samples, seq, width))
        x_out = x_out.reshape(samples, patches // stages, patch_tok, width)
        return x_out, k_new.reshape(k_prev.shape), v_new.reshape(v_prev.shape)

    return jax.shard_map(
        stage_program, mesh=mesh,
        in_specs=(P('dp'), P('dp'), P(), P('pp'), P('pp'), P('pp'), P('pp'), P('pp'), P('pp'), P('pp'), P('pp', 'dp'), P('pp', 'dp')),
        out_specs=(P('dp', 'pp'), P('pp', 'dp'), P('pp', 'dp')),
        check_vma=False)
```

time: 1330 us -> 1060 us (0.80)
  Pallas kernels: 1270 us -> 1010 us
    pallas_call x1, Pallas kernels: 1270 us -> 1010 us  [stage_program(): pl.pallas_call(functools.partial(stage_kernel, stages, UNITS, head_dim),...]
where the time goes in v2:
time: 1060 us
  Pallas kernels  1010 us (95%)
  local copies, waits for them, and re-layouts  29.2 us (3%)
  matrix products  15.8 us (1%)
    pallas_call x1, Pallas kernels, stage_program(): pl.pallas_call(functools.partial(stage_kernel, stages, UNITS, head_dim),...  1010 us
    unnamed x12, local copies, waits for them, and re-layouts  25.1 us

profile of v2, /device:TPU:7, one launch (start us, length us, event | category | flops | bytes accessed | tf_op | source)
XLA Modules:
  0.0 1061.2 jit_solution(8619090098815579817)
XLA Ops:
  0.7 0.7 convert_multiply_fusion.1
  1.4 0.7 tile.29.gains
  2.1 1.3 convert_element_type.41.b_two
  3.4 0.7 copy.23
  4.1 0.1 fusion.12
  4.2 0.8 convert_reduce_fusion
  5.0 1.6 convert.3.b_one
  6.6 15.8 %fusion.2 = f32[3,7296]{1,0:T(4,128)S(1)} fusion(bf16[1,2432,7296]{2,1,0:T(8,128)(2,1)} %param.16, f32[7296]{0:T(1024)S(1)} %convert_reduce_fusion, bf16[3,2432]{1,0:T(4,128)(2,1)} %param.14), kind=kOutput, calls=%fused_computation.2 | convolution fusion | flops 106528896 | bytes 35619072 | tf_op jit(solution)/shard_map/dot_general | solution.py:364
  22.4 0.7 reshape.280.mod
  23.1 0.8 compare_convert_fusion.ones_bd
  23.9 0.1 fusion.10
  24.0 0.4 maximum_cosine_fusion
  24.4 0.5 fusion.14
  24.9 0.2 copy.18
  25.1 0.2 tile.33
  25.3 0.1 broadcast_in_dim.2
  25.4 0.2 tile.30
  25.6 1.0 copy.19.cos_tab
  26.7 1.0 copy.20.sin_tab
  27.7 1009.2 %stage_kernel.1 = (bf16[3,256,2432]{2,1,0:T(8,128)(2,1)}, bf16[3,1024,2432]{2,1,0:T(8,128)(2,1)}, bf16[3,1024,2432]{2,1,0:T(8,128)(2,1)}) custom-call(bf16[3,1024,2432]{2,1,0:T(8,128)(2,1)} %bitcast.44, f32[3,3,2432]{2,1,0:T(4,128)} %reshape.280.mod, f32[7,1,2432]{2,1,0:T(1,128)} %convert.3.b_one, f32[2,1,128]{2,1,0:T(1,128)} %tile.29.gains, ...), custom_call_target="tpu_custom_call" | custom-call | tf_op jit(solution)/shard_map/stage_kernel/pallas_call | solution.py:380
  1036.8 0.0 slice-start
  1036.9 4.3 copy.27
  1041.2 0.0 slice-start.1
  1041.2 0.0 slice-start.2
  1041.2 0.0 slice-start.3
  1041.2 13.1 %copy.28 = bf16[1,3,8,128,2432]{4,3,2,1,0:T(8,128)(2,1)} copy(bf16[1,3,8,128,2432]{4,3,2,1,0:T(8,128)(2,1)} %bitcast.43) | data formatting | bytes 29884416
  1054.3 0.0 slice-done
  1054.3 0.0 slice-done.1
  1054.3 0.0 slice-done.2
  1054.4 1.3 slice-done.3
  1055.7 5.6 copy.29
  (9 shorter events, 0.1 us)
Async XLA Ops:
  1036.8 17.5 %slice-start = ((s8[14942208]{0:T(1024)(128)(4,1)}), s8[2359296]{0:T(1024)(128)(4,1)S(1)}, s32[]{:S(2)}) async-start(s8[14942208]{0:T(1024)(128)(4,1)} %bitcast.40), calls=%async_computation | async-start | bytes 4718592
  1041.2 13.1 %slice-start.1 = ((s8[14942208]{0:T(1024)(128)(4,1)}), s8[4194304]{0:T(1024)(128)(4,1)S(1)}, s32[]{:S(2)}) async-start(s8[14942208]{0:T(1024)(128)(4,1)} %bitcast.40), calls=%async_computation.1 | async-start | bytes 8388608
  1041.2 13.2 %slice-start.2 = ((s8[14942208]{0:T(1024)(128)(4,1)}), s8[4194304]{0:T(1024)(128)(4,1)S(1)}, s32[]{:S(2)}) async-start(s8[14942208]{0:T(1024)(128)(4,1)} %bitcast.40), calls=%async_computation.2 | async-start | bytes 8388608
  1041.2 14.5 %slice-start.3 = ((s8[14942208]{0:T(1024)(128)(4,1)}), s8[4194304]{0:T(1024)(128)(4,1)S(1)}, s32[]{:S(2)}) async-start(s8[14942208]{0:T(1024)(128)(4,1)} %bitcast.40), calls=%async_computation.3 | async-start | bytes 8388608

commit v3 on v2

--- a/solution.py
+++ b/solution.py
@@ -2,6 +2,7 @@
 import math
 import jax
 import jax.numpy as jnp
+import numpy as np
 from jax import lax
 from jax.experimental import pallas as pl
 from jax.experimental.pallas import tpu as pltpu
@@ -13,15 +14,20 @@
 SOFT_ROWS = 16
 
 
-def rope_tables(pos_ids, head_dim):
+def rope_tables(pos_ids, head_dim, lanes):
     axis_zero = head_dim // 8
     axis_rest = (head_dim - axis_zero) // 2
-    pieces = []
+    freqs, axes = [], []
     for axis_idx, axis_dim in enumerate((axis_zero, axis_rest, head_dim - axis_zero - axis_rest)):
-        axis_freqs = 1.0 / (10000.0 ** (jnp.arange(0, axis_dim, 2, dtype=jnp.float32) / axis_dim))
-        pieces.append(pos_ids[..., axis_idx:axis_idx + 1].astype(jnp.float32) * axis_freqs)
-    angles = jnp.concatenate(pieces, axis=-1)
-    return jnp.cos(angles), jnp.sin(angles)
+        freqs.append(1.0 / (10000.0 ** (jnp.arange(0, axis_dim, 2, dtype=jnp.float32) / axis_dim)))
+        axes += [axis_idx] * axis_dim
+    lane_freq = jnp.tile(jnp.repeat(jnp.concatenate(freqs), 2), lanes // head_dim)
+    axis = jnp.array(axes * (lanes // head_dim), jnp.int32)
+    pos = pos_ids.astype(jnp.float32)
+    lane_pos = jnp.where(axis == 0, pos[:, 0:1], jnp.where(axis == 1, pos[:, 1:2], pos[:, 2:3]))
+    angles = lane_pos * lane_freq
+    sign = jnp.where(jnp.arange(lanes) % 2 == 0, -1.0, 1.0)
+    return jnp.cos(angles), jnp.sin(angles) * sign
 
 
 def tile_halves(width):
@@ -155,11 +161,6 @@
             return (pltpu.make_async_copy(k_prev.at[s], k_buf, kv_sem.at[0]),
                     pltpu.make_async_copy(v_prev.at[s], v_buf, kv_sem.at[1]))
 
-        @pl.when(part == 0)
-        def _():
-            for cp in prev_copies():
-                cp.start()
-
         @pl.when(stage == 0)
         def _():
             in_copy(c).wait()
@@ -187,18 +188,28 @@
 
         def proj(weights, j, off, size):
             out = jnp.dot(joined[0], weights[...], preferred_element_type=jnp.float32)
-            return (out + b_one[j, :, pl.ds(off, size)]).astype(jnp.bfloat16)
-
-        def head_tile(j, carry):
-            even = (lax.broadcasted_iota(jnp.int32, (rows, LANES), 1) & 1) == 0
-
-            def rotate(raw, off):
+            return (out + b_one[j, :, pl.ds(off, size)].astype(jnp.float32)).astype(jnp.bfloat16)
+
+        def raw_tile(j, carry):
+            def body(weights, off, size):
+                qkv[j, :, pl.ds(off, size)] = proj(weights, j, off, size)
+
+            run_tile(base + j, body)
+            return carry
+
+        def fresh_copies():
+            return (pltpu.make_async_copy(qkv.at[1], k_new.at[s, span, :], kv_out_sem.at[0]),
+                    pltpu.make_async_copy(qkv.at[2], v_new.at[s, span, :], kv_out_sem.at[1]))
+
+        even = (lax.broadcasted_iota(jnp.int32, (rows, LANES), 1) & 1) == 0
+
+        def head_norm(j):
+            def rotate(off, size):
                 cos_v = cos_tab[span, :]
                 sin_v = sin_tab[span, :]
-                size = raw.shape[1]
                 for lo in range(0, size, 2 * LANES):
                     wide = min(2 * LANES, size - lo)
-                    sub = raw[:, lo:lo + wide].astype(jnp.float32)
+                    sub = qkv[j, :, off + lo:off + lo + wide].astype(jnp.float32)
                     sq = sub * sub
                     ones = ones_bd[:wide, :wide]
                     sq0 = sq.astype(jnp.bfloat16)
@@ -212,42 +223,39 @@
                         rot = one * cos_v + swapped * sin_v
                         qkv[j, :, off + lo + l2:off + lo + l2 + LANES] = rot.astype(jnp.bfloat16)
 
+            return rotate
+
+        def mlp_block(weights, j, lo, off, wide):
+            pre = proj(weights.at[:, pl.ds(lo, wide)], j, off + lo, wide).astype(jnp.float32)
+            joined[j - 2, :, off + lo:off + lo + wide] = jax.nn.gelu(pre, approximate=True).astype(jnp.bfloat16)
+
+        def mlp_head_tile(j, carry):
+            rotate = head_norm(j - 3)
+
             def body(weights, off, size):
-                waiting = None
-                for lo in range(0, size, 4 * LANES):
-                    wide = min(4 * LANES, size - lo)
-                    fresh = (proj(weights.at[:, pl.ds(lo, wide)], j, off + lo, wide), off + lo)
-                    if waiting is not None:
-                        rotate(*waiting)
-                    waiting = fresh
-                rotate(*waiting)
+                rotate(off, size)
+                mlp_block(weights, j, 0, off, size)
 
             run_tile(base + j, body)
             return carry
 
-        lax.fori_loop(0, 2, head_tile, 0)
-
-        def value_body(weights, off, size):
-            qkv[2, :, pl.ds(off, size)] = proj(weights, 2, off, size)
-
-        run_tile(base + 2, value_body)
-
-        def fresh_copies():
-            return (pltpu.make_async_copy(qkv.at[1], k_new.at[s, span, :], kv_out_sem.at[0]),
-                    pltpu.make_async_copy(qkv.at[2], v_new.at[s, span, :], kv_out_sem.at[1]))
+        def mlp_tile(j, carry):
+            run_tile(base + j, lambda weights, off, size: mlp_block(weights, j, 0, off, size))
+            return carry
+
+        lax.fori_loop(0, 3, raw_tile, 0)
+
+        @pl.when(part == 0)
+        def _():
+            for cp in prev_copies():
+                cp.start()
+
+        lax.fori_loop(3, 5, mlp_head_tile, 0)
 
         for cp in fresh_copies():
             cp.start()
 
-        def mlp_tile(j, carry):
-            def body(weights, off, size):
-                pre = proj(weights, j, off, size).astype(jnp.float32)
-                joined[j - 2, :, pl.ds(off, size)] = jax.nn.gelu(pre, approximate=True).astype(jnp.bfloat16)
-
-            run_tile(base + j, body)
-            return carry
-
-        lax.fori_loop(3, tiles_one, mlp_tile, 0)
+        lax.fori_loop(5, tiles_one, mlp_tile, 0)
 
         @pl.when(part == 0)
         def _():
@@ -264,11 +272,11 @@
             quads = -(-pairs // 2)
             two_rows = 2 * patch_tok
 
-            def first_pair(quad):
-                return min(2 * quad, pairs - 2)
+            def filled(quad):
+                return min(2, pairs - 2 * quad)
 
             def score(quad, which, dst):
-                cols = pl.ds((first_pair(quad) + which) * LANES, LANES)
+                cols = pl.ds((2 * quad + which) * LANES, LANES)
                 q2 = qkv[0, q_rows, cols]
                 both = jnp.concatenate([q2 * low_bf, q2 * high_bf], axis=0)
                 dst[...] = lax.dot_general(both, k_buf[:, cols], (((1,), (1,)), ((), ())), preferred_element_type=jnp.float32)
@@ -281,28 +289,27 @@
                     dst[at:at + SOFT_ROWS, :] = (ex * (1.0 / jnp.sum(ex, axis=-1, keepdims=True))).astype(jnp.bfloat16)
 
             def mix(quad, src):
-                cols = pl.ds(first_pair(quad) * LANES, 2 * LANES)
-                mixed = jnp.dot(src[...], v_buf[:, cols], preferred_element_type=jnp.float32)
-                t = patch_tok
-                out = jnp.concatenate([jnp.where(low_half, mixed[:t, :LANES], mixed[t:2 * t, :LANES]),
-                                       jnp.where(low_half, mixed[2 * t:3 * t, LANES:], mixed[3 * t:, LANES:])], axis=1)
-                joined[0, q_rows, cols] = out.astype(jnp.bfloat16)
-
-            def quad_step(quad, before, now):
-                if before is not None:
-                    mix(quad - 1, before)
-                for which, buf in enumerate((score0, score1)):
-                    soften(which, buf, now)
-                    if quad + 1 < quads:
-                        score(quad + 1, which, buf)
-
-            score(0, 0, score0)
-            score(0, 1, score1)
-            quad_step(0, None, prob0)
-
+                count = filled(quad)
+                cols = pl.ds(2 * quad * LANES, count * LANES)
+                mixed = jnp.dot(src[:count * two_rows, :], v_buf[:, cols], preferred_element_type=jnp.float32)
+                for which in range(count):
+                    lanes = slice(which * LANES, (which + 1) * LANES)
+                    top = which * two_rows
+                    out = jnp.where(low_half, mixed[top:top + patch_tok, lanes], mixed[top + patch_tok:top + two_rows, lanes])
+                    joined[0, q_rows, pl.ds((2 * quad + which) * LANES, LANES)] = out.astype(jnp.bfloat16)
+
+            buffers = (score0, score1)
             probs = (prob0, prob1)
-            for quad in range(1, quads):
-                quad_step(quad, probs[1 - quad % 2], probs[quad % 2])
+            for which in range(filled(0)):
+                score(0, which, buffers[which])
+            for quad in range(quads):
+                if quad:
+                    mix(quad - 1, probs[(quad - 1) % 2])
+                for which in range(2):
+                    if which < filled(quad):
+                        soften(which, buffers[which], probs[quad % 2])
+                    if quad + 1 < quads and which < filled(quad + 1):
+                        score(quad + 1, which, buffers[which])
             mix(quads - 1, probs[(quads - 1) % 2])
             return carry
 
@@ -328,7 +335,7 @@
 
         def res_step(r, carry):
             at = pl.ds(pl.multiple_of(r * norm_rows, norm_rows), norm_rows)
-            block_out = acc[at, :] + b_two[...]
+            block_out = acc[at, :] + b_two[...].astype(jnp.float32)
             o_buf[at, :] = (x_now[at, :].astype(jnp.float32) + mod[s, 2:3, :] * block_out).astype(jnp.bfloat16)
             return carry
 
@@ -363,15 +370,12 @@
         cond_act = jax.nn.silu(cond_vec.astype(jnp.float32)).astype(jnp.bfloat16)
         mod = jnp.dot(cond_act, w_mod[0], preferred_element_type=jnp.float32) + b_mod.astype(jnp.float32)
         mod = mod.reshape(samples, 3, width)
-        cos_tab, sin_tab = rope_tables(pos_ids.reshape(seq, 3), head_dim)
+        cos_tab, sin_tab = rope_tables(pos_ids.reshape(seq, 3), head_dim, LANES)
         heads_in_lane = LANES // head_dim
-        cos_tab = jnp.tile(jnp.repeat(cos_tab, 2, axis=-1), (1, heads_in_lane))
-        sin_tab = jnp.stack([-sin_tab, sin_tab], axis=-1).reshape(seq, head_dim)
-        sin_tab = jnp.tile(sin_tab, (1, heads_in_lane))
         scale = jnp.array([1.0 / math.sqrt(head_dim), 1.0], jnp.float32)
         gains = jnp.tile(qk_scale[0].astype(jnp.float32) * scale[:, None], (1, heads_in_lane)).reshape(2, 1, LANES)
-        group = jnp.arange(2 * LANES) // head_dim
-        ones_bd = (group[:, None] == group[None, :]).astype(jnp.bfloat16)
+        group = np.arange(2 * LANES) // head_dim
+        ones_bd = jnp.asarray(group[:, None] == group[None, :], jnp.bfloat16)
         vmem = pl.BlockSpec(memory_space=pltpu.VMEM)
         hbm = pl.BlockSpec(memory_space=pl.ANY)
         act = jax.ShapeDtypeStruct((samples, seq, width), jnp.bfloat16)
@@ -404,8 +408,8 @@
             ],
             compiler_params=pltpu.CompilerParams(collective_id=0, has_side_effects=True, vmem_limit_bytes=67043328),
             name='stage_kernel',
-        )(x_in.reshape(samples, seq, width), mod, b_one.astype(jnp.float32).reshape(tiles_one, 1, width), gains, cos_tab, sin_tab, ones_bd,
-          b_two.astype(jnp.float32), w_one[0], w_two[0], k_prev.reshape(samples, seq, width), v_prev.reshape(samples, seq, width))
+        )(x_in.reshape(samples, seq, width), mod, b_one.reshape(tiles_one, 1, width), gains, cos_tab, sin_tab, ones_bd,
+          b_two, w_one[0], w_two[0], k_prev.reshape(samples, seq, width), v_prev.reshape(samples, seq, width))
         x_out = x_out.reshape(samples, patches // stages, patch_tok, width)
         return x_out, k_new.reshape(k_prev.shape), v_new.reshape(v_prev.shape)
 

time: 1060 us -> 1030 us (0.972)
  Pallas kernels: 1010 us -> 979 us
    pallas_call x1, Pallas kernels: 1010 us -> 979 us  [stage_program(): pl.pallas_call(functools.partial(stage_kernel, stages, UNITS, head_dim),...]
    unnamed x12 -> x16, local copies, waits for them, and re-layouts: 25.1 us -> 24.4 us
where the time goes in v3:
time: 1030 us
  Pallas kernels  979 us (95%)
  local copies, waits for them, and re-layouts  26 us (3%)
  matrix products  15.8 us (2%)
    pallas_call x1, Pallas kernels, stage_program(): pl.pallas_call(functools.partial(stage_kernel, stages, UNITS, head_dim),...  979 us
    unnamed x16, local copies, waits for them, and re-layouts  24.4 us

profile of v3, /device:TPU:7, one launch (start us, length us, event | category | flops | bytes accessed | tf_op | source)
XLA Modules:
  0.0 1027.2 jit_solution(2173328866531714017)
XLA Ops:
  0.7 0.1 pad_maximum_fusion
  0.7 0.7 convert_multiply_fusion.1
  1.5 0.6 tile.16.gains
  2.1 0.7 convert_bitcast_fusion
  2.8 0.1 broadcast_in_dim.59
  2.9 0.1 tile.17
  3.0 0.1 mul.40
  3.1 0.8 convert_reduce_fusion
  3.9 0.0 copy-start
  4.0 0.0 copy-start.1
  4.0 15.8 %fusion.2 = f32[3,7296]{1,0:T(4,128)S(1)} fusion(bf16[1,2432,7296]{2,1,0:T(8,128)(2,1)} %param.18, f32[7296]{0:T(1024)S(1)} %convert_reduce_fusion, bf16[3,2432]{1,0:T(4,128)(2,1)} %param.16), kind=kOutput, calls=%fused_computation.2 | convolution fusion | flops 106528896 | bytes 35619072 | tf_op jit(solution)/shard_map/dot_general | solution.py:371
  19.8 0.7 reshape.70.mod
  20.5 0.0 copy-done
  20.5 0.0 copy-done.1
  20.5 3.5 sine_multiply_fusion
  24.0 978.8 %stage_kernel.1 = (bf16[3,256,2432]{2,1,0:T(8,128)(2,1)}, bf16[3,1024,2432]{2,1,0:T(8,128)(2,1)}, bf16[3,1024,2432]{2,1,0:T(8,128)(2,1)}) custom-call(bf16[3,1024,2432]{2,1,0:T(8,128)(2,1)} %bitcast.32, f32[3,3,2432]{2,1,0:T(4,128)} %reshape.70.mod, bf16[7,1,2432]{2,1,0:T(2,128)(2,1)} %bitcast.36, f32[2,1,128]{2,1,0:T(1,128)} %tile.16.gains, ...), custom_call_target="tpu_custom_call" | custom-call | tf_op jit(solution)/shard_map/stage_kernel/pallas_call | solution.py:384
  1002.8 0.0 slice-start
  1002.8 4.3 copy.24
  1007.1 0.0 slice-start.1
  1007.1 0.0 slice-start.2
  1007.1 0.0 slice-start.3
  1007.1 13.1 %copy.25 = bf16[1,3,8,128,2432]{4,3,2,1,0:T(8,128)(2,1)} copy(bf16[1,3,8,128,2432]{4,3,2,1,0:T(8,128)(2,1)} %bitcast.31) | data formatting | bytes 29884416
  1020.3 0.0 slice-done
  1020.3 0.0 slice-done.1
  1020.3 0.0 slice-done.2
  1020.3 1.3 slice-done.3
  1021.6 5.6 copy.26
  (8 shorter events, 0.1 us)
Async XLA Ops:
  3.9 16.6 %copy-start = (pred[128]{0:T(512)(128)(4,1)S(1)}, pred[128]{0:T(512)(128)(4,1)}, u32[]{:S(2)}) copy-start(pred[128]{0:T(512)(128)(4,1)} %constant.60) | copy-start | bytes 388
  4.0 16.5 %copy-start.1 = (pred[128]{0:T(512)(128)(4,1)S(1)}, pred[128]{0:T(512)(128)(4,1)}, u32[]{:S(2)}) copy-start(pred[128]{0:T(512)(128)(4,1)} %constant.59) | copy-start | bytes 388
  1002.8 17.5 %slice-start = ((s8[14942208]{0:T(1024)(128)(4,1)}), s8[2359296]{0:T(1024)(128)(4,1)S(1)}, s32[]{:S(2)}) async-start(s8[14942208]{0:T(1024)(128)(4,1)} %bitcast.28), calls=%async_computation | async-start | bytes 4718592
  1007.1 13.1 %slice-start.1 = ((s8[14942208]{0:T(1024)(128)(4,1)}), s8[4194304]{0:T(1024)(128)(4,1)S(1)}, s32[]{:S(2)}) async-start(s8[14942208]{0:T(1024)(128)(4,1)} %bitcast.28), calls=%async_computation.1 | async-start | bytes 8388608
  1007.1 13.2 %slice-start.2 = ((s8[14942208]{0:T(1024)(128)(4,1)}), s8[4194304]{0:T(1024)(128)(4,1)S(1)}, s32[]{:S(2)}) async-start(s8[14942208]{0:T(1024)(128)(4,1)} %bitcast.28), calls=%async_computation.2 | async-start | bytes 8388608
  1007.1 14.5 %slice-start.3 = ((s8[14942208]{0:T(1024)(128)(4,1)}), s8[4194304]{0:T(1024)(128)(4,1)S(1)}, s32[]{:S(2)}) async-start(s8[14942208]{0:T(1024)(128)(4,1)} %bitcast.28), calls=%async_computation.3 | async-start | bytes 8388608
